TPU v7x, 32 devices: a whole 2x2x4 slice. The times are simulated.
32 devices in a mesh: tm: 4 (over y, x), orig: 8 (over z, core).
Axes of the slice: x: 2, y: 2, z: 4, core: 2. Of those that a mesh axis runs over, the one named last changes fastest.
Arguments:
- trip_counts: bfloat16 [12, 96, 256, 256], P('tm', 'orig'), may hold values from 0.25 to 4
- anchor_hour: float32 [12, 2048], P('tm', 'orig'), may hold values from 100 to 3000
- dest_hour: float32 [12, 32768], P('tm'), may hold values from 100 to 3000
- daily_target: bfloat16 [96, 256, 256], P('orig'), may hold values from 2 to 40
- block_columns: int32 [96], P('orig'), may hold values from -1 to 127, as said below
Outputs:
- fitted: bfloat16 [12, 96, 256, 256], P('tm', 'orig')
- dest_gap: float32 [12, 32768], P('tm', 'orig')
Inputs may be any that keep to these rules, and one draw needn't show every extreme that they name: `block_columns`: within each anchor block row the live column numbers are distinct and come first, followed by -1 for empty slots; every block row has at least one live slot, and some block row has all 12 live.
All inputs are finite; a program needn't handle non-finite values.
Results may differ from a plain program's by a relative error of at most 0.001.
Values sent between devices are 32-bit elements; how exact they have to be, the bound alone decides.
No kernel may reach another device: no remote copies, remote signals or barrier semaphores. Data moves between devices by JAX's collectives and lax.ppermute only.
A program may use at most 64 MiB of HBM per device.

v0:
```python
import functools

import jax
import jax.numpy as jnp
from jax import lax
from jax.experimental import pallas as pl
from jax.experimental.pallas import tpu as pltpu
from jax.sharding import PartitionSpec as P


LANES = 128
F32 = jnp.float32
LIMIT = pltpu.CompilerParams(vmem_limit_bytes=8 * 2**20)


def whole(memory_space=pltpu.VMEM):
    return pl.BlockSpec(memory_space=memory_space)


def near(*xs):
    return [pltpu.with_memory_space_constraint(x, pltpu.VMEM) for x in xs]


def far(*xs):
    return [pltpu.with_memory_space_constraint(x, pltpu.HBM) for x in xs]


def anchor_kernel(place, cols, anchor, trips, local, acol, sums, pick, margins, arrivals, *, starts):
    bins, slots, side, _ = trips.shape
    halves = side // LANES
    rows = side // 4
    first = pltpu.make_async_copy(anchor, margins, arrivals.at[4 * bins])
    first.start()
    blocks = [(t, r) for t in range(bins) for r in range(0, side, rows)]
    copies = [
        pltpu.make_async_copy(trips.at[t, :, r : r + rows, :], local.at[t, :, r : r + rows, :], arrivals.at[i])
        for i, (t, r) in enumerate(blocks)
    ]
    for copy in copies:
        copy.start()
    pick[0] = functools.reduce(lambda a, b: a + b, [(cols[s] >= 0).astype(jnp.int32) for s in starts])
    count = bins * halves * slots
    for s in range(slots):
        sums[count + s : count + s + 1, :] = jnp.full((1, LANES), cols[s], jnp.int32).astype(F32)
    live = [(cols[s] >= 0).astype(F32) for s in range(slots)]
    first.wait()
    acc = None
    for copy, (t, r) in zip(copies, blocks):
        copy.wait()
        if r == 0:
            acc = [[None] * halves for _ in range(slots)]
        total = None
        for s in range(slots):
            part = local[t, s, r : r + rows, :].astype(F32) * live[s]
            total = part if total is None else total + part
        total = jnp.sum(total, axis=1, keepdims=True)
        diagonal = (
            lax.broadcasted_iota(jnp.int32, (rows, side), 0) + r == lax.broadcasted_iota(jnp.int32, (rows, side), 1)
        )
        column = jnp.sum(jnp.where(diagonal, margins[t : t + 1, :], 0.0), axis=1, keepdims=True)
        scale = jnp.broadcast_to(column / total, (rows, LANES))
        acol[t, r : r + rows, :] = scale
        for s in range(slots):
            for h in range(halves):
                part = local[t, s, r : r + rows, h * LANES : (h + 1) * LANES].astype(F32) * scale
                part = jnp.sum(part.reshape(rows // 8, 8, LANES), axis=0)
                acc[s][h] = part if acc[s][h] is None else acc[s][h] + part
        if r + rows == side:
            for h in range(halves):
                for s in range(slots):
                    row = (t * halves + h) * slots + s
                    sums[row : row + 1, :] = jnp.sum(acc[s][h], axis=0, keepdims=True)


def lookup_kernel(place, cols, dest, picked, span):
    parts, slots, _ = picked.shape
    bins = dest.shape[0]
    halves = parts // bins
    side = halves * LANES
    for s in range(slots):
        start = pl.multiple_of(jnp.maximum(cols[s], 0) * side, side)
        row = dest[:, pl.ds(start, side)]
        for t in range(bins):
            for h in range(halves):
                picked[t * halves + h, s : s + 1, :] = row[t : t + 1, h * LANES : (h + 1) * LANES]
    width = span.shape[1]
    span[...] = dest[:, pl.ds(pl.multiple_of(place[1] * width, width), width)]


def matched(own, columns, values, parts, slots, first):
    acc = [jnp.zeros(own.shape, F32) for _ in range(parts)]
    at = 0
    for vref in values:
        for k in range(vref.shape[0]):
            cref, c = (vref, k) if columns is None else (columns, at)
            at += 1
            for s in range(slots):
                hit = own == cref[c, first + s : first + s + 1, :]
                for q in range(parts):
                    acc[q] = acc[q] + jnp.where(hit, vref[k, q * slots + s : q * slots + s + 1, :], 0.0)
    return acc


def gap_kernel(place, span, *refs):
    out = refs[-1]
    columns, values = refs[0], refs[1:-1]
    slots = columns.shape[1]
    first = values[0].shape[1]
    parts = first // slots
    bins = out.shape[0]
    halves = parts // bins
    side = halves * LANES
    blocks = out.shape[1] // side
    own = (lax.broadcasted_iota(jnp.int32, (blocks, LANES), 0) + place[1] * blocks).astype(F32)
    total = matched(own, columns, values, parts, slots, 0)
    for t in range(bins):
        for h in range(halves):
            for c in range(blocks):
                at = c * side + h * LANES
                out[t : t + 1, at : at + LANES] = total[t * halves + h][c : c + 1, :]
    out[...] = out[...] / span[...] - 1.0


def blocks_of(place, kept):
    first, second = place[0] >> 1, place[0] & 1
    if kept:
        return first, 2 + second
    return 1 - first, 3 - second


def rows_of(block, rows):
    return pl.ds(pl.multiple_of(block * rows, rows), rows)


def day_kernel(place, trips, acol, picked, *refs, ranges, count):
    arrived, gain, columns, outs = refs[:count], refs[count], refs[count + 1], refs[count + 2 :]
    bins, slots, side, _ = trips.shape
    halves = side // LANES
    rows = side // 4
    parts = bins * halves
    first = parts * slots
    own = arrived[0][0, first : first + slots, :]
    total = matched(own, None, arrived, parts, slots, first)
    for q in range(parts):
        gain[q] = jnp.where(own >= 0.0, picked[q] / jnp.maximum(total[q], 1.0), 0.0)
    at = 0
    for ref in arrived:
        for k in range(ref.shape[0]):
            columns[at] = ref[k, first : first + slots, :]
            at += 1
    for kept in (False, True):
        for k, block in enumerate(blocks_of(place, kept)):
            at = rows_of(block, rows)
            scale = [acol[t, at, :] for t in range(bins)]
            for r, (start, n) in enumerate(ranges):
                out = outs[4 * r + 2 * kept + k]
                for i in range(n):
                    for h in range(halves):
                        lanes = slice(h * LANES, (h + 1) * LANES)
                        acc = None
                        for t in range(bins):
                            q = t * halves + h
                            part = trips[t, start + i, at, lanes].astype(F32) * scale[t]
                            part = part * gain[q, start + i : start + i + 1, :]
                            acc = part if acc is None else acc + part
                        out[i, :, lanes] = acc


def factor_kernel(place, cols, target, *refs, start):
    ins, outs = refs[:-2], refs[-2:]
    count, rows, _ = outs[0].shape
    for k, block in enumerate(blocks_of(place, True)):
        for i in range(count):
            empty = (cols[start + i] < 0).astype(F32)
            wanted = target[start + i, rows_of(block, rows), :].astype(F32)
            outs[k][i] = wanted / (ins[2 * k][i] + ins[2 * k + 1][i] + empty)


def fit_rows(place, trips, acol, gain, fa, fb, sums_in, local, sums, start, kept):
    bins, slots, side, _ = trips.shape
    halves = side // LANES
    count, rows, _ = fa.shape
    sums[...] = sums_in[...]
    places = [rows_of(block, rows) for block in blocks_of(place, kept)]
    scale = [[acol[t, at, :] for t in range(bins)] for at in places]
    for i in range(count):
        for t in range(bins):
            for h in range(halves):
                lanes = slice(h * LANES, (h + 1) * LANES)
                q = t * halves + h
                g = gain[q, start + i : start + i + 1, :]
                total = None
                for k, (at, factor) in enumerate(zip(places, (fa, fb))):
                    value = trips[t, start + i, at, lanes].astype(F32) * scale[k][t] * g * factor[i, :, lanes]
                    local[t, i, at, lanes] = value.astype(local.dtype)
                    part = jnp.sum(value.reshape(rows // 8, 8, LANES), axis=0)
                    total = part if total is None else total + part
                row = q * slots + start + i
                sums[row : row + 1, :] = sums[row : row + 1, :] + jnp.sum(total, axis=0, keepdims=True)


def kept_kernel(place, trips, acol, gain, fa, fb, sums_in, local, sums, *, start):
    fit_rows(place, trips, acol, gain, fa, fb, sums_in, local, sums, start, True)


def rest_kernel(place, trips, acol, gain, fa, fb, sums_in, mine, *refs, start, before, empty, last, chained):
    refs = list(refs)
    ready = refs.pop(0) if before is not None else None
    if chained:
        refs.pop(0)
    local, sums = refs[:2]
    fitted, blank, done = refs[2:] if len(refs) > 2 else (None, None, None)
    bins, count, _, _ = local.shape
    copies = []

    def put(source, target):
        copies.append(pltpu.make_async_copy(source, target, done.at[len(copies)]))
        copies[-1].start()

    if empty:
        blank[...] = jnp.zeros(blank.shape, blank.dtype)
    for t in range(bins):
        if before is not None:
            put(ready.at[t], fitted.at[t, before[0] : before[0] + before[1]])
        for s in empty:
            put(blank, fitted.at[t, s])
    fit_rows(place, trips, acol, gain, fa, fb, sums_in, local, sums, start, False)
    if last:
        for t in range(bins):
            put(local.at[t], fitted.at[t, start : start + count])
    for copy in copies:
        copy.wait()


def cycle(trips, acol, gain, target, cols, place, days, *, ranges):
    bins, slots, side, _ = trips.shape
    halves = side // LANES
    rows = side // 4
    parts = bins * halves
    used = sum(count for _, count in ranges)
    groups = ranges[::-1]
    days = [days[4 * r : 4 * r + 4] for r in range(len(ranges))][::-1]

    def over_first(x):
        return lax.ppermute(x, "tm", [(i, i ^ 2) for i in range(4)])

    def over_second(x):
        return lax.ppermute(x, "tm", [(i, i ^ 1) for i in range(4)])

    def factor(start, count, *sums):
        shape = pltpu.VMEM((count, rows, side), F32)
        return pl.pallas_call(
            functools.partial(factor_kernel, start=start),
            compiler_params=LIMIT,
            in_specs=[whole(pltpu.SMEM)] * 2 + [whole()] * 5,
            out_specs=[whole(), whole()],
            out_shape=[shape, shape],
        )(place, cols, *near(target, *sums))

    def fit_kept(start, count, fa, fb, sums):
        return pl.pallas_call(
            functools.partial(kept_kernel, start=start),
            compiler_params=LIMIT,
            in_specs=[whole(pltpu.SMEM)] + [whole()] * 6,
            out_specs=[whole(), whole()],
            out_shape=[pltpu.VMEM((bins, count, side, side), trips.dtype), pltpu.VMEM((parts * slots, LANES), F32)],
        )(place, *near(trips, acol, gain, fa, fb, sums))

    def fit_rest(start, count, fa, fb, sums, mine, before, ready, fitted, last):
        empty = range(used, slots) if fitted is None and before is None else ()
        if len(groups) > 1 and used == slots:
            empty = ()
        writes = before is not None or len(empty) > 0 or last
        extra = near(ready) if before is not None else []
        aliases = {7: 0}
        if fitted is not None:
            aliases[8 + len(extra)] = 2
            extra = extra + far(fitted)
        in_specs = [whole(pltpu.SMEM)] + [whole()] * 7 + [whole()] * (before is not None)
        in_specs += [whole(pltpu.HBM)] * (fitted is not None)
        copies = bins * ((before is not None) + len(empty) + last)
        outs = pl.pallas_call(
            functools.partial(
                rest_kernel, start=start, before=before, empty=empty, last=last, chained=fitted is not None
            ),
            compiler_params=LIMIT,
            in_specs=in_specs,
            out_specs=[whole(), whole()] + [whole(pltpu.HBM)] * writes,
            out_shape=[pltpu.VMEM((bins, count, side, side), trips.dtype), pltpu.VMEM((parts * slots, LANES), F32)]
            + [pltpu.HBM(trips.shape, trips.dtype)] * writes,
            scratch_shapes=[pltpu.VMEM((side, side), trips.dtype), pltpu.SemaphoreType.DMA((copies,))] * writes,
            input_output_aliases=aliases,
        )(place, *near(trips, acol, gain, fa, fb, sums, mine), *extra)
        return outs if writes else [*outs, None]

    order = range(len(groups))
    got = [(over_first(days[g][0]), over_second(days[g][1])) for g in order]
    mine = [(d[2] + g[0], d[3] + g[1]) for d, g in zip(days, got)]
    other = [(over_second(mine[g][0]), over_first(mine[g][1])) for g in order]
    scale = [factor(s, n, m[0], o[0], m[1], o[1]) for (s, n), m, o in zip(groups, mine, other)]
    back = [(over_first(scale[g][0]), over_second(scale[g][1])) for g in order]
    sums = jnp.zeros((parts * slots, LANES), F32)
    before = ready = fitted = None
    for i, ((s, n), f, b) in enumerate(zip(groups, scale, back)):
        local, sums = fit_kept(s, n, f[0], f[1], sums)
        ready, sums, fitted = fit_rest(
            s, n, b[0], b[1], sums, local, before, ready, fitted, i == len(groups) - 1
        )
        before = (s, n)
    return fitted, sums


def gather(x, n, beside):
    def swap(y, k):
        return lax.ppermute(y, "orig", [(i, i ^ k) for i in range(n)])

    distant = [swap(x, k) for k in range(n - 2, 0, -2)]
    distant, beside = lax.optimization_barrier((distant, beside))
    close = jnp.stack([x] + distant)
    return [close, swap(close, 1)], beside


def make(mesh):
    n_orig = mesh.shape["orig"]
    n_tm = mesh.shape["tm"]
    assert n_tm == 4 and n_orig & (n_orig - 1) == 0 and n_orig > 1

    def on_device(trip_counts, anchor_hour, dest_hour, daily_target, block_columns):
        bins, slots, side, _ = trip_counts.shape
        halves = side // LANES
        parts = bins * halves
        width = dest_hour.shape[1] // n_orig
        place = jnp.stack([lax.axis_index("tm").astype(jnp.int32), lax.axis_index("orig").astype(jnp.int32)])
        place, block_columns = lax.optimization_barrier((place, block_columns))

        cuts = [max(slots // 6, 1), max(slots // 2, 2), slots]
        ranges = [(a, b - a) for a, b in zip([0] + cuts, cuts)]
        local, acol, sums, pick = pl.pallas_call(
            functools.partial(anchor_kernel, starts=cuts[:-1]),
            compiler_params=LIMIT,
            in_specs=[whole(pltpu.SMEM), whole(pltpu.SMEM), whole(pltpu.HBM), whole(pltpu.HBM)],
            out_specs=[whole(), whole(), whole(), whole(pltpu.SMEM)],
            out_shape=[
                pltpu.VMEM(trip_counts.shape, trip_counts.dtype),
                pltpu.VMEM((bins, side, LANES), F32),
                pltpu.VMEM(((parts + 1) * slots, LANES), F32),
                jax.ShapeDtypeStruct((1,), jnp.int32),
            ],
            scratch_shapes=[pltpu.VMEM((bins, side), F32), pltpu.SemaphoreType.DMA((4 * bins + 1,))],
        )(place, block_columns, *far(anchor_hour, trip_counts))

        picked, span = pl.pallas_call(
            lookup_kernel,
            compiler_params=LIMIT,
            in_specs=[whole(pltpu.SMEM), whole(pltpu.SMEM), whole()],
            out_specs=[whole(), whole()],
            out_shape=[
                pltpu.VMEM((parts, slots, LANES), F32),
                pltpu.VMEM((bins, width), F32),
            ],
        )(place, block_columns, dest_hour)
        arrived, picked = gather(sums, n_orig, picked)

        quarter = side // 4
        gain, columns, *days = pl.pallas_call(
            functools.partial(day_kernel, ranges=ranges, count=len(arrived)),
            compiler_params=LIMIT,
            in_specs=[whole(pltpu.SMEM)] + [whole()] * (3 + len(arrived)),
            out_specs=[whole()] * (2 + 4 * len(ranges)),
            out_shape=[
                pltpu.VMEM((parts, slots, LANES), F32),
                pltpu.VMEM((n_orig, slots, LANES), F32),
            ]
            + [pltpu.VMEM((n, quarter, side), F32) for _, n in ranges for _ in range(4)],
        )(place, *near(local, acol, picked, *arrived))

        def branch(k):
            def run(*args):
                return cycle(*args, ranges=ranges[: k + 1])

            return run

        days, pick = lax.optimization_barrier((days, pick))
        fitted, final = lax.switch(
            pick[0],
            [branch(k) for k in range(len(ranges))],
            local,
            acol,
            gain,
            daily_target,
            block_columns,
            place,
            days,
        )
        fitted, final = lax.optimization_barrier((fitted, final))
        finals, _ = gather(final, n_orig, place)
        gap = pl.pallas_call(
            gap_kernel,
            compiler_params=LIMIT,
            in_specs=[whole(pltpu.SMEM), whole(), whole()] + [whole()] * len(finals),
            out_specs=whole(),
            out_shape=jax.ShapeDtypeStruct((bins, width), F32),
        )(place, *near(span, columns, *finals))
        return fitted, gap

    return on_device


def solution(mesh):
    placed = (
        P("tm", "orig", None, None),
        P("tm", "orig"),
        P("tm", None),
        P("orig", None, None),
        P("orig"),
    )
    return jax.shard_map(
        make(mesh),
        mesh=mesh,
        in_specs=placed,
        out_specs=(P("tm", "orig", None, None), P("tm", "orig")),
        check_vma=False,
    )
```

profile of v0, /device:TPU:0, one launch (start us, length us, event | category | flops | bytes accessed | tf_op | source)
XLA Modules:
  0.0 86.8 jit_solution(8018987987645946466)
XLA Ops:
  0.7 4.9 %shard_map.68 = (bf16[3,12,256,256]{3,2,1,0:T(8,128)(2,1)S(1)}, f32[3,256,128]{2,1,0:T(8,128)S(1)}, f32[84,128]{1,0:T(8,128)S(1)}, s32[1]{0:T(128)}) custom-call(s32[2]{0:T(128)S(1)} %pad_add_fusion.place, s32[12]{0:T(128)} %cols.1, f32[3,256]{1,0:T(4,128)} %anchor.1, bf16[3,12,256,256]{3,2,1,0:T(8,128)(2,1)} %trips.1), custom_call_target="tpu_custom_call" | custom-call | tf_op jit(solution)/shard_map/pallas_call | solution.py:338
  5.6 3.1 %collective-permute-start.38 = (f32[84,128]{1,0:T(8,128)S(1)}, f32[84,128]{1,0:T(8,128)S(1)}, u32[]{:S(2)}, u32[]{:S(2)}) collective-permute-start(f32[84,128]{1,0:T(8,128)S(1)} %get-tuple-element.214), channel_id=1, source_target_pairs={{0,2},{1,3},{2,0},{3,1},{4,6},{5,7},{6,4},{7,5},{8,10},{9,11},{10,... | collective-permute-start | bytes 129032 | tf_op jit(solution)/shard_map/ppermute | solution.py:315
  8.7 2.6 %collective-permute-start.37 = (f32[84,128]{1,0:T(8,128)S(1)}, f32[84,128]{1,0:T(8,128)S(1)}, u32[]{:S(2)}, u32[]{:S(2)}) collective-permute-start(f32[84,128]{1,0:T(8,128)S(1)} %get-tuple-element.214), channel_id=1, source_target_pairs={{0,4},{1,5},{2,6},{3,7},{4,0},{5,1},{6,2},{7,3},{8,12},{9,13},{10,... | collective-permute-start | bytes 129032 | tf_op jit(solution)/shard_map/ppermute | solution.py:315
  11.9 2.6 %collective-permute-done.37 = f32[84,128]{1,0:T(8,128)S(1)} collective-permute-done((f32[84,128]{1,0:T(8,128)S(1)}, f32[84,128]{1,0:T(8,128)S(1)}, u32[]{:S(2)}, u32[]{:S(2)}) %collective-permute-start.37) | collective-permute-done | bytes 43040 | tf_op jit(solution)/shard_map/ppermute | solution.py:315
  14.5 2.6 %collective-permute-done.36 = f32[84,128]{1,0:T(8,128)S(1)} collective-permute-done((f32[84,128]{1,0:T(8,128)S(1)}, f32[84,128]{1,0:T(8,128)S(1)}, u32[]{:S(2)}, u32[]{:S(2)}) %collective-permute-start.36) | collective-permute-done | bytes 43040 | tf_op jit(solution)/shard_map/ppermute | solution.py:315
  17.3 1.4 %collective-permute-done.39.refs_1_ = f32[4,84,128]{2,1,0:T(8,128)S(1)} collective-permute-done((f32[4,84,128]{2,1,0:T(8,128)S(1)}, f32[4,84,128]{2,1,0:T(8,128)S(1)}, u32[]{:S(2)}, u32[]{:S(2)}) %collective-permute-start.39) | collective-permute-done | bytes 172064 | tf_op jit(solution)/shard_map/ppermute | solution.py:315
  18.7 2.1 %shard_map.70 = (f32[6,12,128]{2,1,0:T(8,128)S(1)}, f32[8,12,128]{2,1,0:T(8,128)S(1)}, f32[2,64,256]{2,1,0:T(8,128)S(1)}, f32[2,64,256]{2,1,0:T(8,128)S(1)}, f32...) custom-call(s32[2]{0:T(128)S(1)} %pad_add_fusion.place, ...), custom_call_target="tpu_custom_call" | custom-call | tf_op jit(solution)/shard_map/pallas_call | solution.py:365
  21.4 36.9 %conditional.1 = (bf16[3,12,256,256]{3,2,1,0:T(8,128)(2,1)}, f32[72,128]{1,0:T(8,128)S(1)}) conditional(s32[]{:T(128)} %bitcast.6, (f32[2,64,256]{2,1,0:T(8,128)S(1)}, f32[2,64,256]{2,1,0:T(8,128)S(1)}, f32[2,64,256]{2,1,0:T(8,128)S(1)}, f32[2,64,256]{2,1,0:T(8,128)S(1)}, s32[2]{0:T(128)S(1)}, /*index=5*/s32[12]{0:T(128)S(1)}, ...), branch_computations={%region_0.0_spmd, %region_1.0_spmd, %region_2.0_spmd} | conditional | flops 393216 | bytes 23630564 | solution.py:384
  21.4 1.6 %collective-permute-start.12 = (f32[4,64,256]{2,1,0:T(8,128)S(1)}, f32[4,64,256]{2,1,0:T(8,128)S(1)}, u32[]{:S(2)}, u32[]{:S(2)}) collective-permute-start(f32[4,64,256]{2,1,0:T(8,128)S(1)} %get-tuple-element.113), channel_id=1, source_target_pairs={{0,16},{8,24},{16,0},{24,8},{1,17},{9,25},{17,1},{25,9},{2,18},{10... | collective-permute-start | bytes 786440 | tf_op jit(solution)/shard_map/cond/branch_1_fun/ppermute | solution.py:245
  23.0 1.5 %collective-permute-start.14 = (f32[4,64,256]{2,1,0:T(8,128)S(1)}, f32[4,64,256]{2,1,0:T(8,128)S(1)}, u32[]{:S(2)}, u32[]{:S(2)}) collective-permute-start(f32[4,64,256]{2,1,0:T(8,128)S(1)} %get-tuple-element.115), channel_id=1, source_target_pairs={{0,8},{8,0},{16,24},{24,16},{1,9},{9,1},{17,25},{25,17},{2,10},{10... | collective-permute-start | bytes 786440 | tf_op jit(solution)/shard_map/cond/branch_1_fun/ppermute | solution.py:248
  24.5 3.9 %collective-permute-done.12 = f32[4,64,256]{2,1,0:T(8,128)S(1)} collective-permute-done((f32[4,64,256]{2,1,0:T(8,128)S(1)}, f32[4,64,256]{2,1,0:T(8,128)S(1)}, u32[]{:S(2)}, u32[]{:S(2)}) %collective-permute-start.12) | collective-permute-done | bytes 262176 | tf_op jit(solution)/shard_map/cond/branch_1_fun/ppermute | solution.py:245
  28.4 1.6 %collective-permute-start.13 = (f32[4,64,256]{2,1,0:T(8,128)S(1)}, f32[4,64,256]{2,1,0:T(8,128)S(1)}, u32[]{:S(2)}, u32[]{:S(2)}) collective-permute-start(f32[4,64,256]{2,1,0:T(8,128)S(1)} %add.28.refs_0_), channel_id=1, source_target_pairs={{0,8},{8,0},{16,24},{24,16},{1,9},{9,1},{17,25},{25,17},{2,10},{10... | collective-permute-start | bytes 786440 | tf_op jit(solution)/shard_map/cond/branch_1_fun/ppermute | solution.py:248
  32.5 1.5 %collective-permute-start.8 = (f32[2,64,256]{2,1,0:T(8,128)S(1)}, f32[2,64,256]{2,1,0:T(8,128)S(1)}, u32[]{:S(2)}, u32[]{:S(2)}) collective-permute-start(f32[2,64,256]{2,1,0:T(8,128)S(1)} %get-tuple-element.109), channel_id=1, source_target_pairs={{0,8},{8,0},{16,24},{24,16},{1,9},{9,1},{17,25},{25,17},{2,10},{10... | collective-permute-start | bytes 393224 | tf_op jit(solution)/shard_map/cond/branch_1_fun/ppermute | solution.py:248
  34.0 5.7 %collective-permute-done.6 = f32[2,64,256]{2,1,0:T(8,128)S(1)} collective-permute-done((f32[2,64,256]{2,1,0:T(8,128)S(1)}, f32[2,64,256]{2,1,0:T(8,128)S(1)}, u32[]{:S(2)}, u32[]{:S(2)}) %collective-permute-start.6) | collective-permute-done | bytes 131104 | tf_op jit(solution)/shard_map/cond/branch_1_fun/ppermute | solution.py:245
  39.6 1.6 %collective-permute-start.7 = (f32[2,64,256]{2,1,0:T(8,128)S(1)}, f32[2,64,256]{2,1,0:T(8,128)S(1)}, u32[]{:S(2)}, u32[]{:S(2)}) collective-permute-start(f32[2,64,256]{2,1,0:T(8,128)S(1)} %add.26.refs_0_), channel_id=1, source_target_pairs={{0,8},{8,0},{16,24},{24,16},{1,9},{9,1},{17,25},{25,17},{2,10},{10... | collective-permute-start | bytes 393224 | tf_op jit(solution)/shard_map/cond/branch_1_fun/ppermute | solution.py:248
  42.1 1.5 %collective-permute-start.17 = (f32[4,64,256]{2,1,0:T(8,128)S(1)}, f32[4,64,256]{2,1,0:T(8,128)S(1)}, u32[]{:S(2)}, u32[]{:S(2)}) collective-permute-start(f32[4,64,256]{2,1,0:T(8,128)S(1)} %get-tuple-element.117.fb), channel_id=1, source_target_pairs={{0,8},{8,0},{16,24},{24,16},{1,9},{9,1},{17,25},{25,17},{2,10},{10... | collective-permute-start | bytes 786440 | tf_op jit(solution)/shard_map/cond/branch_1_fun/ppermute | solution.py:248
  44.7 5.0 %collective-permute-done.9.refs_3_ = f32[2,64,256]{2,1,0:T(8,128)S(1)} collective-permute-done((f32[2,64,256]{2,1,0:T(8,128)S(1)}, f32[2,64,256]{2,1,0:T(8,128)S(1)}, u32[]{:S(2)}, u32[]{:S(2)}) %collective-permute-start.9) | collective-permute-done | bytes 131104 | tf_op jit(solution)/shard_map/cond/branch_1_fun/ppermute | solution.py:245
  50.6 1.5 %collective-permute-start.11 = (f32[2,64,256]{2,1,0:T(8,128)S(1)}, f32[2,64,256]{2,1,0:T(8,128)S(1)}, u32[]{:S(2)}, u32[]{:S(2)}) collective-permute-start(f32[2,64,256]{2,1,0:T(8,128)S(1)} %get-tuple-element.111.fb), channel_id=1, source_target_pairs={{0,8},{8,0},{16,24},{24,16},{1,9},{9,1},{17,25},{25,17},{2,10},{10... | collective-permute-start | bytes 393224 | tf_op jit(solution)/shard_map/cond/branch_1_fun/ppermute | solution.py:248
  53.0 2.1 %branch_1_fun.9 = (bf16[3,4,256,256]{3,2,1,0:T(8,128)(2,1)S(1)}, f32[72,128]{1,0:T(8,128)S(1)}, bf16[3,12,256,256]{3,2,1,0:T(8,128)(2,1)}) custom-call(s32[2]{0:T(128)S(1)} %get-tuple-element.100.place, bf16[3,12,256,256]{3,2,1,0:T(8,128)(2,1)S(1)} %get-tuple-element.101.trips, ...), custom_call_target="tpu_custom_call", output_to_operand_aliasing={{0}: (7, {})} | custom-call | tf_op jit(solution)/shard_map/cond/branch_1_fun/pallas_call | solution.py:282
  55.9 2.0 %branch_1_fun.11 = (bf16[3,2,256,256]{3,2,1,0:T(8,128)(2,1)S(1)}, f32[72,128]{1,0:T(8,128)S(1)}, bf16[3,12,256,256]{3,2,1,0:T(8,128)(2,1)}) custom-call(s32[2]{0:T(128)S(1)} %get-tuple-element.100.place, bf16[3,12,256,256]{3,2,1,0:T(8,128)(2,1)S(1)} %get-tuple-element.101.trips, ...), custom_call_target="tpu_custom_call", output_to_operand_aliasing={{0}: (7, {}), {2}: (9, {})} | custom-call | tf_op jit(solution)/shard_map/cond/branch_1_fun/pallas_call | solution.py:282
  58.4 19.7 %collective-permute-start.41 = (f32[72,128]{1,0:T(8,128)S(1)}, f32[72,128]{1,0:T(8,128)S(1)}, u32[]{:S(2)}, u32[]{:S(2)}) collective-permute-start(f32[72,128]{1,0:T(8,128)S(1)} %get-tuple-element.250), channel_id=1, source_target_pairs={{0,4},{1,5},{2,6},{3,7},{4,0},{5,1},{6,2},{7,3},{8,12},{9,13},{10,... | collective-permute-start | bytes 110600 | tf_op jit(solution)/shard_map/ppermute | solution.py:315
  78.6 1.5 %collective-permute-done.41 = f32[72,128]{1,0:T(8,128)S(1)} collective-permute-done((f32[72,128]{1,0:T(8,128)S(1)}, f32[72,128]{1,0:T(8,128)S(1)}, u32[]{:S(2)}, u32[]{:S(2)}) %collective-permute-start.41) | collective-permute-done | bytes 36896 | tf_op jit(solution)/shard_map/ppermute | solution.py:315
  80.0 3.8 %collective-permute-done.40 = f32[72,128]{1,0:T(8,128)S(1)} collective-permute-done((f32[72,128]{1,0:T(8,128)S(1)}, f32[72,128]{1,0:T(8,128)S(1)}, u32[]{:S(2)}, u32[]{:S(2)}) %collective-permute-start.40) | collective-permute-done | bytes 36896 | tf_op jit(solution)/shard_map/ppermute | solution.py:315
  85.3 1.5 %shard_map.71 = f32[3,4096]{1,0:T(4,128)} custom-call(s32[2]{0:T(128)S(1)} %pad_add_fusion.place, f32[3,4096]{1,0:T(4,128)S(1)} %get-tuple-element.248.span, f32[8,12,128]{2,1,0:T(8,128)S(1)} %get-tuple-element.249.refs_0_, f32[4,72,128]{2,1,0:T(8,128)S(1)} %pad_maximum_fusion.1.refs_1_, f32[4,72,128]{2,1,0:T(8,128)S(1)} %collective-permute-done.43.refs_2_), custom_call_target="tpu_custom_call" | custom-call | tf_op jit(solution)/shard_map/pallas_call | solution.py:397
  (41 shorter events, 9.8 us)
Async XLA Ops:
  0.6 10.7 %copy-start.2 = (s32[12]{0:T(128)S(1)}, s32[12]{0:T(128)}, u32[]{:S(2)}) copy-start(s32[12]{0:T(128)} %cols.1) | copy-start | bytes 148
  0.6 10.7 %copy-start.1 = (f32[3,32768]{1,0:T(4,128)S(1)}, f32[3,32768]{1,0:T(4,128)}, u32[]{:S(2)}) copy-start(f32[3,32768]{1,0:T(4,128)} %dest.1) | copy-start | bytes 1179652
  0.7 20.6 %copy-start = (bf16[12,256,256]{2,1,0:T(8,128)(2,1)S(1)}, bf16[12,256,256]{2,1,0:T(8,128)(2,1)}, u32[]{:S(2)}) copy-start(bf16[12,256,256]{2,1,0:T(8,128)(2,1)} %param.11) | copy-start | bytes 4718596
  5.6 6.3 %collective-permute-start.38 = (f32[84,128]{1,0:T(8,128)S(1)}, f32[84,128]{1,0:T(8,128)S(1)}, u32[]{:S(2)}, u32[]{:S(2)}) collective-permute-start(f32[84,128]{1,0:T(8,128)S(1)} %get-tuple-element.214), channel_id=1, source_target_pairs={{0,2},{1,3},{2,0},{3,1},{4,6},{5,7},{6,4},{7,5},{8,10},{9,11},{10,... | collective-permute-start | bytes 129032 | tf_op jit(solution)/shard_map/ppermute | solution.py:315
  8.7 5.8 %collective-permute-start.37 = (f32[84,128]{1,0:T(8,128)S(1)}, f32[84,128]{1,0:T(8,128)S(1)}, u32[]{:S(2)}, u32[]{:S(2)}) collective-permute-start(f32[84,128]{1,0:T(8,128)S(1)} %get-tuple-element.214), channel_id=1, source_target_pairs={{0,4},{1,5},{2,6},{3,7},{4,0},{5,1},{6,2},{7,3},{8,12},{9,13},{10,... | collective-permute-start | bytes 129032 | tf_op jit(solution)/shard_map/ppermute | solution.py:315
  11.3 5.8 %collective-permute-start.36 = (f32[84,128]{1,0:T(8,128)S(1)}, f32[84,128]{1,0:T(8,128)S(1)}, u32[]{:S(2)}, u32[]{:S(2)}) collective-permute-start(f32[84,128]{1,0:T(8,128)S(1)} %get-tuple-element.214), channel_id=1, source_target_pairs={{0,6},{1,7},{2,4},{3,5},{4,2},{5,3},{6,0},{7,1},{8,14},{9,15},{10,... | collective-permute-start | bytes 129032 | tf_op jit(solution)/shard_map/ppermute | solution.py:315
  17.2 1.5 %collective-permute-start.39 = (f32[4,84,128]{2,1,0:T(8,128)S(1)}, f32[4,84,128]{2,1,0:T(8,128)S(1)}, u32[]{:S(2)}, u32[]{:S(2)}) collective-permute-start(f32[4,84,128]{2,1,0:T(8,128)S(1)} %pad_maximum_fusion.refs_0_), channel_id=1, source_target_pairs={{0,1},{1,0},{2,3},{3,2},{4,5},{5,4},{6,7},{7,6},{8,9},{9,8},{10,11... | collective-permute-start | bytes 516104 | tf_op jit(solution)/shard_map/ppermute | solution.py:315
  21.4 7.0 %collective-permute-start.12 = (f32[4,64,256]{2,1,0:T(8,128)S(1)}, f32[4,64,256]{2,1,0:T(8,128)S(1)}, u32[]{:S(2)}, u32[]{:S(2)}) collective-permute-start(f32[4,64,256]{2,1,0:T(8,128)S(1)} %get-tuple-element.113), channel_id=1, source_target_pairs={{0,16},{8,24},{16,0},{24,8},{1,17},{9,25},{17,1},{25,9},{2,18},{10... | collective-permute-start | bytes 786440 | tf_op jit(solution)/shard_map/cond/branch_1_fun/ppermute | solution.py:245
  23.0 7.3 %collective-permute-start.14 = (f32[4,64,256]{2,1,0:T(8,128)S(1)}, f32[4,64,256]{2,1,0:T(8,128)S(1)}, u32[]{:S(2)}, u32[]{:S(2)}) collective-permute-start(f32[4,64,256]{2,1,0:T(8,128)S(1)} %get-tuple-element.115), channel_id=1, source_target_pairs={{0,8},{8,0},{16,24},{24,16},{1,9},{9,1},{17,25},{25,17},{2,10},{10... | collective-permute-start | bytes 786440 | tf_op jit(solution)/shard_map/cond/branch_1_fun/ppermute | solution.py:248
  28.4 12.8 %collective-permute-start.13 = (f32[4,64,256]{2,1,0:T(8,128)S(1)}, f32[4,64,256]{2,1,0:T(8,128)S(1)}, u32[]{:S(2)}, u32[]{:S(2)}) collective-permute-start(f32[4,64,256]{2,1,0:T(8,128)S(1)} %add.28.refs_0_), channel_id=1, source_target_pairs={{0,8},{8,0},{16,24},{24,16},{1,9},{9,1},{17,25},{25,17},{2,10},{10... | collective-permute-start | bytes 786440 | tf_op jit(solution)/shard_map/cond/branch_1_fun/ppermute | solution.py:248
  30.4 10.8 %collective-permute-start.15 = (f32[4,64,256]{2,1,0:T(8,128)S(1)}, f32[4,64,256]{2,1,0:T(8,128)S(1)}, u32[]{:S(2)}, u32[]{:S(2)}) collective-permute-start(f32[4,64,256]{2,1,0:T(8,128)S(1)} %add.29.refs_2_), channel_id=1, source_target_pairs={{0,16},{8,24},{16,0},{24,8},{1,17},{9,25},{17,1},{25,9},{2,18},{10... | collective-permute-start | bytes 786440 | tf_op jit(solution)/shard_map/cond/branch_1_fun/ppermute | solution.py:245
  31.6 8.0 %collective-permute-start.6 = (f32[2,64,256]{2,1,0:T(8,128)S(1)}, f32[2,64,256]{2,1,0:T(8,128)S(1)}, u32[]{:S(2)}, u32[]{:S(2)}) collective-permute-start(f32[2,64,256]{2,1,0:T(8,128)S(1)} %get-tuple-element.107), channel_id=1, source_target_pairs={{0,16},{8,24},{16,0},{24,8},{1,17},{9,25},{17,1},{25,9},{2,18},{10... | collective-permute-start | bytes 393224 | tf_op jit(solution)/shard_map/cond/branch_1_fun/ppermute | solution.py:245
  32.5 11.2 %collective-permute-start.8 = (f32[2,64,256]{2,1,0:T(8,128)S(1)}, f32[2,64,256]{2,1,0:T(8,128)S(1)}, u32[]{:S(2)}, u32[]{:S(2)}) collective-permute-start(f32[2,64,256]{2,1,0:T(8,128)S(1)} %get-tuple-element.109), channel_id=1, source_target_pairs={{0,8},{8,0},{16,24},{24,16},{1,9},{9,1},{17,25},{25,17},{2,10},{10... | collective-permute-start | bytes 393224 | tf_op jit(solution)/shard_map/cond/branch_1_fun/ppermute | solution.py:248
  39.6 5.0 %collective-permute-start.7 = (f32[2,64,256]{2,1,0:T(8,128)S(1)}, f32[2,64,256]{2,1,0:T(8,128)S(1)}, u32[]{:S(2)}, u32[]{:S(2)}) collective-permute-start(f32[2,64,256]{2,1,0:T(8,128)S(1)} %add.26.refs_0_), channel_id=1, source_target_pairs={{0,8},{8,0},{16,24},{24,16},{1,9},{9,1},{17,25},{25,17},{2,10},{10... | collective-permute-start | bytes 393224 | tf_op jit(solution)/shard_map/cond/branch_1_fun/ppermute | solution.py:248
  41.9 11.1 %collective-permute-start.16 = (f32[4,64,256]{2,1,0:T(8,128)S(1)}, f32[4,64,256]{2,1,0:T(8,128)S(1)}, u32[]{:S(2)}, u32[]{:S(2)}) collective-permute-start(f32[4,64,256]{2,1,0:T(8,128)S(1)} %get-tuple-element.116.fa), channel_id=1, source_target_pairs={{0,16},{8,24},{16,0},{24,8},{1,17},{9,25},{17,1},{25,9},{2,18},{10... | collective-permute-start | bytes 786440 | tf_op jit(solution)/shard_map/cond/branch_1_fun/ppermute | solution.py:245
  42.1 10.9 %collective-permute-start.17 = (f32[4,64,256]{2,1,0:T(8,128)S(1)}, f32[4,64,256]{2,1,0:T(8,128)S(1)}, u32[]{:S(2)}, u32[]{:S(2)}) collective-permute-start(f32[4,64,256]{2,1,0:T(8,128)S(1)} %get-tuple-element.117.fb), channel_id=1, source_target_pairs={{0,8},{8,0},{16,24},{24,16},{1,9},{9,1},{17,25},{25,17},{2,10},{10... | collective-permute-start | bytes 786440 | tf_op jit(solution)/shard_map/cond/branch_1_fun/ppermute | solution.py:248
  43.7 6.0 %collective-permute-start.9 = (f32[2,64,256]{2,1,0:T(8,128)S(1)}, f32[2,64,256]{2,1,0:T(8,128)S(1)}, u32[]{:S(2)}, u32[]{:S(2)}) collective-permute-start(f32[2,64,256]{2,1,0:T(8,128)S(1)} %add.27.refs_2_), channel_id=1, source_target_pairs={{0,16},{8,24},{16,0},{24,8},{1,17},{9,25},{17,1},{25,9},{2,18},{10... | collective-permute-start | bytes 393224 | tf_op jit(solution)/shard_map/cond/branch_1_fun/ppermute | solution.py:245
  50.3 5.5 %collective-permute-start.10 = (f32[2,64,256]{2,1,0:T(8,128)S(1)}, f32[2,64,256]{2,1,0:T(8,128)S(1)}, u32[]{:S(2)}, u32[]{:S(2)}) collective-permute-start(f32[2,64,256]{2,1,0:T(8,128)S(1)} %get-tuple-element.110.fa), channel_id=1, source_target_pairs={{0,16},{8,24},{16,0},{24,8},{1,17},{9,25},{17,1},{25,9},{2,18},{10... | collective-permute-start | bytes 393224 | tf_op jit(solution)/shard_map/cond/branch_1_fun/ppermute | solution.py:245
  50.6 5.3 %collective-permute-start.11 = (f32[2,64,256]{2,1,0:T(8,128)S(1)}, f32[2,64,256]{2,1,0:T(8,128)S(1)}, u32[]{:S(2)}, u32[]{:S(2)}) collective-permute-start(f32[2,64,256]{2,1,0:T(8,128)S(1)} %get-tuple-element.111.fb), channel_id=1, source_target_pairs={{0,8},{8,0},{16,24},{24,16},{1,9},{9,1},{17,25},{25,17},{2,10},{10... | collective-permute-start | bytes 393224 | tf_op jit(solution)/shard_map/cond/branch_1_fun/ppermute | solution.py:248
  58.3 20.3 %collective-permute-start.42 = (f32[72,128]{1,0:T(8,128)S(1)}, f32[72,128]{1,0:T(8,128)S(1)}, u32[]{:S(2)}, u32[]{:S(2)}) collective-permute-start(f32[72,128]{1,0:T(8,128)S(1)} %get-tuple-element.250), channel_id=1, source_target_pairs={{0,2},{1,3},{2,0},{3,1},{4,6},{5,7},{6,4},{7,5},{8,10},{9,11},{10,... | collective-permute-start | bytes 110600 | tf_op jit(solution)/shard_map/ppermute | solution.py:315
  58.4 21.7 %collective-permute-start.41 = (f32[72,128]{1,0:T(8,128)S(1)}, f32[72,128]{1,0:T(8,128)S(1)}, u32[]{:S(2)}, u32[]{:S(2)}) collective-permute-start(f32[72,128]{1,0:T(8,128)S(1)} %get-tuple-element.250), channel_id=1, source_target_pairs={{0,4},{1,5},{2,6},{3,7},{4,0},{5,1},{6,2},{7,3},{8,12},{9,13},{10,... | collective-permute-start | bytes 110600 | tf_op jit(solution)/shard_map/ppermute | solution.py:315
  78.1 5.8 %collective-permute-start.40 = (f32[72,128]{1,0:T(8,128)S(1)}, f32[72,128]{1,0:T(8,128)S(1)}, u32[]{:S(2)}, u32[]{:S(2)}) collective-permute-start(f32[72,128]{1,0:T(8,128)S(1)} %get-tuple-element.250), channel_id=1, source_target_pairs={{0,6},{1,7},{2,4},{3,5},{4,2},{5,3},{6,0},{7,1},{8,14},{9,15},{10,... | collective-permute-start | bytes 110600 | tf_op jit(solution)/shard_map/ppermute | solution.py:315
  83.8 1.4 %collective-permute-start.43 = (f32[4,72,128]{2,1,0:T(8,128)S(1)}, f32[4,72,128]{2,1,0:T(8,128)S(1)}, u32[]{:S(2)}, u32[]{:S(2)}) collective-permute-start(f32[4,72,128]{2,1,0:T(8,128)S(1)} %pad_maximum_fusion.1.refs_1_), channel_id=1, source_target_pairs={{0,1},{1,0},{2,3},{3,2},{4,5},{5,4},{6,7},{7,6},{8,9},{9,8},{10,11... | collective-permute-start | bytes 442376 | tf_op jit(solution)/shard_map/ppermute | solution.py:315
where the time goes:
time: 87 us; the launch traced here: 86.8 us
  starting transfers between devices  40.4 us (46%)
  waiting for transfers between devices  28.3 us (33%)
  Pallas kernels  16 us (18%)
  between operations  1.38 us (2%)
    ppermute x8, starting transfers between devices, swap(): return lax.ppermute(y, 'orig', [(i, i ^ k) for i in range(n)])  26.1 us
    ppermute x6, waiting for transfers between devices, over_first(): return lax.ppermute(x, 'tm', [(i, i ^ 2) for i in range(4)])  14.6 us
    ppermute x8, waiting for transfers between devices, swap(): return lax.ppermute(y, 'orig', [(i, i ^ k) for i in range(n)])  13.3 us
    ppermute x6, starting transfers between devices, over_second(): return lax.ppermute(x, 'tm', [(i, i ^ 1) for i in range(4)])  9.08 us
    ppermute x6, starting transfers between devices, over_first(): return lax.ppermute(x, 'tm', [(i, i ^ 2) for i in range(4)])  5.17 us
    pallas_call x1, Pallas kernels, on_device(): pl.pallas_call(functools.partial(anchor_kernel, starts=cuts[:-1]), compil...  4.86 us
    pallas_call x2, Pallas kernels, fit_rest(): pl.pallas_call(functools.partial(rest_kernel, start=start, before=before,...  4.08 us
    pallas_call x1, Pallas kernels, on_device(): pl.pallas_call(functools.partial(day_kernel, ranges=ranges, count=len(arr...  2.05 us
  transfers between devices with their start and end apart: 20, of which 11 were waited for; matrix products, arithmetic and copies ran while one was open for 0% of the time, Pallas kernels for 6%

commit v1 on v0

v1 whole, which is shorter than its diff:
```python
import functools

import jax
import jax.numpy as jnp
from jax import lax
from jax.experimental import pallas as pl
from jax.experimental.pallas import tpu as pltpu
from jax.sharding import PartitionSpec as P


LANES = 128
F32 = jnp.float32
LIMIT = pltpu.CompilerParams(vmem_limit_bytes=8 * 2**20)


def whole(memory_space=pltpu.VMEM):
    return pl.BlockSpec(memory_space=memory_space)


def near(*xs):
    return [pltpu.with_memory_space_constraint(x, pltpu.VMEM) for x in xs]


def far(*xs):
    return [pltpu.with_memory_space_constraint(x, pltpu.HBM) for x in xs]


def anchor_kernel(place, cols, anchor, trips, local, acol, sums, pick, margins, arrivals, *, starts):
    bins, slots, side, _ = trips.shape
    halves = side // LANES
    rows = side // 4
    first = pltpu.make_async_copy(anchor, margins, arrivals.at[4 * bins])
    first.start()
    blocks = [(t, r) for t in range(bins) for r in range(0, side, rows)]
    copies = [
        pltpu.make_async_copy(trips.at[t, :, r : r + rows, :], local.at[t, :, r : r + rows, :], arrivals.at[i])
        for i, (t, r) in enumerate(blocks)
    ]
    for copy in copies:
        copy.start()
    pick[0] = functools.reduce(lambda a, b: a + b, [(cols[s] >= 0).astype(jnp.int32) for s in starts])
    count = bins * halves * slots
    for s in range(slots):
        sums[count + s : count + s + 1, :] = jnp.full((1, LANES), cols[s], jnp.int32).astype(F32)
    live = [(cols[s] >= 0).astype(F32) for s in range(slots)]
    first.wait()
    for t, r in blocks:
        diagonal = (
            lax.broadcasted_iota(jnp.int32, (rows, side), 0) + r == lax.broadcasted_iota(jnp.int32, (rows, side), 1)
        )
        column = jnp.sum(jnp.where(diagonal, margins[t : t + 1, :], 0.0), axis=1, keepdims=True)
        acol[t, r : r + rows, :] = jnp.broadcast_to(column, (rows, LANES))

    def row_totals(t, r):
        total = None
        for s in range(slots):
            part = local[t, s, r : r + rows, :].astype(F32) * live[s]
            total = part if total is None else total + part
        return jnp.sum(total, axis=1, keepdims=True)

    def column_sums(t, r, total, acc):
        scale = acol[t, r : r + rows, :] / jnp.broadcast_to(total, (rows, LANES))
        acol[t, r : r + rows, :] = scale
        for s in range(slots):
            for h in range(halves):
                part = local[t, s, r : r + rows, h * LANES : (h + 1) * LANES].astype(F32) * scale
                part = jnp.sum(part.reshape(rows // 8, 8, LANES), axis=0)
                acc[s][h] = part if r == 0 else acc[s][h] + part
        if r + rows == side:
            for h in range(halves):
                for s in range(slots):
                    row = (t * halves + h) * slots + s
                    sums[row : row + 1, :] = jnp.sum(acc[s][h], axis=0, keepdims=True)

    acc = [[None] * halves for _ in range(slots)]
    waiting = None
    for copy, (t, r) in zip(copies, blocks):
        copy.wait()
        total = row_totals(t, r)
        if waiting is not None:
            column_sums(*waiting, acc)
        waiting = (t, r, total)
    column_sums(*waiting, acc)


def lookup_kernel(place, cols, dest, target, picked, span, *wanted, ranges):
    parts, slots, _ = picked.shape
    bins = dest.shape[0]
    halves = parts // bins
    side = halves * LANES
    for s in range(slots):
        start = pl.multiple_of(jnp.maximum(cols[s], 0) * side, side)
        row = dest[:, pl.ds(start, side)]
        for t in range(bins):
            for h in range(halves):
                picked[t * halves + h, s : s + 1, :] = row[t : t + 1, h * LANES : (h + 1) * LANES]
    width = span.shape[1]
    span[...] = dest[:, pl.ds(pl.multiple_of(place[1] * width, width), width)]
    for r, (start, count) in enumerate(ranges):
        for k, block in enumerate(blocks_of(place, True)):
            out = wanted[2 * r + k]
            out[...] = target[start : start + count, rows_of(block, out.shape[1]), :].astype(F32)


def matched(own, columns, values, parts, slots, first):
    acc = [jnp.zeros(own.shape, F32) for _ in range(parts)]
    at = 0
    for vref in values:
        for k in range(vref.shape[0]):
            cref, c = (vref, k) if columns is None else (columns, at)
            at += 1
            for s in range(slots):
                hit = own == cref[c, first + s : first + s + 1, :]
                for q in range(parts):
                    acc[q] = acc[q] + jnp.where(hit, vref[k, q * slots + s : q * slots + s + 1, :], 0.0)
    return acc


def gap_kernel(place, span, *refs):
    out = refs[-1]
    columns, values = refs[0], refs[1:-1]
    slots = columns.shape[1]
    first = values[0].shape[1]
    parts = first // slots
    bins = out.shape[0]
    halves = parts // bins
    side = halves * LANES
    blocks = out.shape[1] // side
    own = (lax.broadcasted_iota(jnp.int32, (blocks, LANES), 0) + place[1] * blocks).astype(F32)
    total = matched(own, columns, values, parts, slots, 0)
    for t in range(bins):
        for h in range(halves):
            for c in range(blocks):
                at = c * side + h * LANES
                out[t : t + 1, at : at + LANES] = total[t * halves + h][c : c + 1, :]
    out[...] = out[...] / span[...] - 1.0


def blocks_of(place, kept):
    first, second = place[0] >> 1, place[0] & 1
    if kept:
        return first, 2 + second
    return 1 - first, 3 - second


def rows_of(block, rows):
    return pl.ds(pl.multiple_of(block * rows, rows), rows)


def day_kernel(place, trips, acol, picked, *refs, ranges, count):
    arrived, gain, columns, first_trips, outs = refs[:count], refs[count], refs[count + 1], refs[count + 2], refs[count + 3 :]
    first_trips[...] = trips[:, : first_trips.shape[1]]
    bins, slots, side, _ = trips.shape
    halves = side // LANES
    parts = bins * halves
    first = parts * slots
    own = arrived[0][0, first : first + slots, :]
    total = matched(own, None, arrived, parts, slots, first)
    for q in range(parts):
        gain[q] = jnp.where(own >= 0.0, picked[q] / jnp.maximum(total[q], 1.0), 0.0)
    at = 0
    for ref in arrived:
        for k in range(ref.shape[0]):
            columns[at] = ref[k, first : first + slots, :]
            at += 1
    day_parts(place, trips, acol, gain, outs, ranges, False)


def keep_kernel(place, trips, acol, gain, *outs, ranges):
    day_parts(place, trips, acol, gain, outs, ranges, True)


def day_parts(place, trips, acol, gain, outs, ranges, kept):
    bins, _, side, _ = trips.shape
    halves = side // LANES
    rows = side // 4
    for k, block in enumerate(blocks_of(place, kept)):
        at = rows_of(block, rows)
        scale = [acol[t, at, :] for t in range(bins)]
        for r, (start, n) in enumerate(ranges):
            out = outs[2 * r + k]
            for i in range(n):
                for h in range(halves):
                    lanes = slice(h * LANES, (h + 1) * LANES)
                    acc = None
                    for t in range(bins):
                        q = t * halves + h
                        part = trips[t, start + i, at, lanes].astype(F32) * scale[t]
                        part = part * gain[q, start + i : start + i + 1, :]
                        acc = part if acc is None else acc + part
                    out[i, :, lanes] = acc


def fit_rows(place, trips, acol, gain, fa, fb, local, sums, start, kept):
    bins, _, side, _ = trips.shape
    slots = gain.shape[1]
    halves = side // LANES
    count, rows, _ = fa.shape
    places = [rows_of(block, rows) for block in blocks_of(place, kept)]
    scale = [[acol[t, at, :] for t in range(bins)] for at in places]
    for i in range(count):
        for t in range(bins):
            for h in range(halves):
                lanes = slice(h * LANES, (h + 1) * LANES)
                q = t * halves + h
                g = gain[q, start + i : start + i + 1, :]
                total = None
                for k, (at, factor) in enumerate(zip(places, (fa, fb))):
                    value = trips[t, start + i, at, lanes].astype(F32) * scale[k][t] * g * factor[i, :, lanes]
                    local[t, i, at, lanes] = value.astype(local.dtype)
                    part = jnp.sum(value.reshape(rows // 8, 8, LANES), axis=0)
                    total = part if total is None else total + part
                row = q * slots + start + i
                total = jnp.sum(total, axis=0, keepdims=True)
                sums[row : row + 1, :] = total if kept else sums[row : row + 1, :] + total


def copy_all(pairs, done):
    copies = [pltpu.make_async_copy(source, target, done.at[i]) for i, (source, target) in enumerate(pairs)]
    for copy in copies:
        copy.start()
    return copies


def copy_all(pairs, done, first=0):
    copies = [pltpu.make_async_copy(source, target, done.at[first + i]) for i, (source, target) in enumerate(pairs)]
    for copy in copies:
        copy.start()
    return copies


def empty_kernel(sums, fitted, blank, done, *, empty):
    sums[...] = jnp.zeros(sums.shape, F32)
    blank[...] = jnp.zeros(blank.shape, blank.dtype)
    for copy in copy_all([(blank, fitted.at[t, s]) for t in range(fitted.shape[0]) for s in empty], done):
        copy.wait()


def kept_kernel(place, trips, acol, gain, sums_in, *refs, ranges):
    n = len(ranges)
    factors, locals_, sums = refs[: 2 * n], refs[2 * n : 3 * n], refs[3 * n]
    sums[...] = sums_in[...]
    for r, (start, _) in enumerate(ranges):
        fit_rows(place, trips, acol, gain, factors[2 * r], factors[2 * r + 1], locals_[r], sums, start, True)


def rest_kernel(place, trips, acol, gain, fa, fb, sums_in, mine, *refs, start, ready_start, chained, last):
    refs = list(refs)
    ready = refs.pop(0) if ready_start is not None else None
    if chained:
        refs.pop(0)
    local, sums = refs[:2]
    bins, count, _, _ = local.shape
    copies = []
    if ready is not None:
        fitted, done = refs[2:]
        pairs = [(ready.at[t], fitted.at[t, ready_start : ready_start + ready.shape[1]]) for t in range(bins)]
        copies += copy_all(pairs, done)
    sums[...] = sums_in[...]
    fit_rows(place, trips, acol, gain, fa, fb, local, sums, start, False)
    if last:
        fitted, done = refs[2:]
        copies += copy_all([(local.at[t], fitted.at[t, start : start + count]) for t in range(bins)], done, len(copies))
    for copy in copies:
        copy.wait()


def end_kernel(place, trips, acol, gain, fa, fb, ga, gb, sums_in, local, sums, *, start):
    sums[...] = sums_in[...]
    fit_rows(place, trips, acol, gain, fa, fb, local, sums, start, True)
    fit_rows(place, trips, acol, gain, ga, gb, local, sums, start, False)


def store_kernel(local, before, fitted, done, *, start):
    bins, count, _, _ = local.shape
    for copy in copy_all([(local.at[t], fitted.at[t, start : start + count]) for t in range(bins)], done):
        copy.wait()


def cycle(trips, acol, gain, cols, place, wanted, sends, *, ranges, used):
    bins, slots, side, _ = trips.shape
    halves = side // LANES
    rows = side // 4
    parts = bins * halves
    order = range(used)[::-1]

    def over_first(x):
        return lax.ppermute(x, "tm", [(i, i ^ 2) for i in range(4)])

    def over_second(x):
        return lax.ppermute(x, "tm", [(i, i ^ 1) for i in range(4)])

    def factor(r, k, mine, other):
        start, count = ranges[r]
        empty = (cols[start : start + count] < 0).astype(F32)[:, None, None]
        return wanted[2 * r + k] / (mine + other + empty)

    def total(kept, got):
        return kept + got

    got = {r: (over_first(sends[2 * r]), over_second(sends[2 * r + 1])) for r in order}
    kept = pl.pallas_call(
        functools.partial(keep_kernel, ranges=ranges[:used]),
        compiler_params=LIMIT,
        in_specs=[whole(pltpu.SMEM)] + [whole()] * 3,
        out_specs=[whole()] * (2 * used),
        out_shape=[pltpu.VMEM((n, rows, side), F32) for _, n in ranges[:used] for _ in range(2)],
    )(place, *near(trips, acol, gain))
    mine = {r: [total(kept[2 * r + k], got[r][k]) for k in range(2)] for r in order}
    other = {r: (over_second(mine[r][0]), over_first(mine[r][1])) for r in order}
    scale = {r: [factor(r, k, mine[r][k], other[r][k]) for k in range(2)] for r in order}
    back = {r: (over_first(scale[r][0]), over_second(scale[r][1])) for r in order}
    shapes = [pltpu.VMEM((bins, n, side, side), trips.dtype) for _, n in ranges]
    final = pltpu.VMEM((parts * slots, LANES), F32)
    store = pltpu.HBM(trips.shape, trips.dtype)
    sums, fitted = jnp.zeros((parts * slots, LANES), F32), None
    if used < len(ranges):
        empty = range(ranges[used][0], slots)
        sums, fitted = pl.pallas_call(
            functools.partial(empty_kernel, empty=empty),
            compiler_params=LIMIT,
            out_specs=[whole(), whole(pltpu.HBM)],
            out_shape=[final, store],
            scratch_shapes=[pltpu.VMEM((side, side), trips.dtype), pltpu.SemaphoreType.DMA((bins * len(empty),))],
        )()
    if used > 1:
        *out, sums = pl.pallas_call(
            functools.partial(kept_kernel, ranges=ranges[1:used]),
            compiler_params=LIMIT,
            in_specs=[whole(pltpu.SMEM)] + [whole()] * (4 + 2 * (used - 1)),
            out_specs=[whole()] * used,
            out_shape=[*shapes[1:used], final],
        )(place, *near(trips, acol, gain, sums, *[f for r in range(1, used) for f in scale[r]]))
        out = [None] + out
    for r in order[:-1]:
        ready = [out[r + 1]] if r + 1 < used else []
        last = r == 1
        writes = len(ready) + last
        chain = far(fitted) if writes and fitted is not None else []
        outs = pl.pallas_call(
            functools.partial(
                rest_kernel,
                start=ranges[r][0],
                ready_start=ranges[r + 1][0] if ready else None,
                chained=len(chain) > 0,
                last=last,
            ),
            compiler_params=LIMIT,
            in_specs=[whole(pltpu.SMEM)] + [whole()] * (7 + len(ready)) + [whole(pltpu.HBM)] * len(chain),
            out_specs=[whole(), whole()] + [whole(pltpu.HBM)] * (writes > 0),
            out_shape=[shapes[r], final] + [store] * (writes > 0),
            scratch_shapes=[pltpu.SemaphoreType.DMA((bins * writes,))] * (writes > 0),
            input_output_aliases={7: 0} | ({8 + len(ready): 2} if chain else {}),
        )(place, *near(trips, acol, gain, *back[r], sums, out[r], *ready), *chain)
        out[r], sums = outs[:2]
        if writes:
            fitted = outs[2]
    return [*scale[0], *back[0]], sums, fitted


def gather(x, n, beside):
    def swap(y, k):
        return lax.ppermute(y, "orig", [(i, i ^ k) for i in range(n)])

    distant = [swap(x, k) for k in range(n - 2, 0, -2)]
    distant, beside = lax.optimization_barrier((distant, beside))
    close = jnp.stack([x] + distant)
    return [close, swap(close, 1)], beside


def make(mesh):
    n_orig = mesh.shape["orig"]
    n_tm = mesh.shape["tm"]
    assert n_tm == 4 and n_orig & (n_orig - 1) == 0 and n_orig > 1

    def on_device(trip_counts, anchor_hour, dest_hour, daily_target, block_columns):
        bins, slots, side, _ = trip_counts.shape
        halves = side // LANES
        parts = bins * halves
        width = dest_hour.shape[1] // n_orig
        place = jnp.stack([lax.axis_index("tm").astype(jnp.int32), lax.axis_index("orig").astype(jnp.int32)])
        place, block_columns = lax.optimization_barrier((place, block_columns))

        cuts = [max(slots // 6, 1), max(slots // 2, 2), slots]
        ranges = [(a, b - a) for a, b in zip([0] + cuts, cuts)]
        local, acol, sums, pick = pl.pallas_call(
            functools.partial(anchor_kernel, starts=cuts[:-1]),
            compiler_params=LIMIT,
            in_specs=[whole(pltpu.SMEM), whole(pltpu.SMEM), whole(pltpu.HBM), whole(pltpu.HBM)],
            out_specs=[whole(), whole(), whole(), whole(pltpu.SMEM)],
            out_shape=[
                pltpu.VMEM(trip_counts.shape, trip_counts.dtype),
                pltpu.VMEM((bins, side, LANES), F32),
                pltpu.VMEM(((parts + 1) * slots, LANES), F32),
                jax.ShapeDtypeStruct((1,), jnp.int32),
            ],
            scratch_shapes=[pltpu.VMEM((bins, side), F32), pltpu.SemaphoreType.DMA((4 * bins + 1,))],
        )(place, block_columns, *far(anchor_hour, trip_counts))

        picked, span, *wanted = pl.pallas_call(
            functools.partial(lookup_kernel, ranges=ranges),
            compiler_params=LIMIT,
            in_specs=[whole(pltpu.SMEM), whole(pltpu.SMEM), whole(), whole()],
            out_specs=[whole()] * (2 + 2 * len(ranges)),
            out_shape=[
                pltpu.VMEM((parts, slots, LANES), F32),
                pltpu.VMEM((bins, width), F32),
            ]
            + [pltpu.VMEM((n, side // 4, side), F32) for _, n in ranges for _ in range(2)],
        )(place, block_columns, *near(dest_hour, daily_target))
        arrived, picked = gather(sums, n_orig, picked)

        quarter = side // 4
        gain, columns, opening, *sends = pl.pallas_call(
            functools.partial(day_kernel, ranges=ranges, count=len(arrived)),
            compiler_params=LIMIT,
            in_specs=[whole(pltpu.SMEM)] + [whole()] * (3 + len(arrived)),
            out_specs=[whole()] * (3 + 2 * len(ranges)),
            out_shape=[
                pltpu.VMEM((parts, slots, LANES), F32),
                pltpu.VMEM((n_orig, slots, LANES), F32),
                pltpu.VMEM((bins, ranges[0][1], side, side), trip_counts.dtype),
            ]
            + [pltpu.VMEM((n, quarter, side), F32) for _, n in ranges for _ in range(2)],
        )(place, *near(local, acol, picked, *arrived))

        def branch(k):
            def run(*args):
                return cycle(*args, ranges=ranges, used=k + 1)

            return run

        factors, final, fitted = lax.switch(
            pick[0],
            [branch(k) for k in range(len(ranges))],
            local,
            acol,
            gain,
            block_columns,
            place,
            wanted,
            sends,
        )
        block, final = pl.pallas_call(
            functools.partial(end_kernel, start=ranges[0][0]),
            compiler_params=LIMIT,
            in_specs=[whole(pltpu.SMEM)] + [whole()] * 8,
            out_specs=[whole(), whole()],
            out_shape=[
                pltpu.VMEM((bins, ranges[0][1], side, side), trip_counts.dtype),
                pltpu.VMEM((parts * slots, LANES), F32),
            ],
        )(place, *near(opening, acol, gain, *factors, final))
        fitted = pl.pallas_call(
            functools.partial(store_kernel, start=ranges[0][0]),
            compiler_params=LIMIT,
            in_specs=[whole(), whole(pltpu.HBM)],
            out_specs=whole(pltpu.HBM),
            out_shape=pltpu.HBM(trip_counts.shape, trip_counts.dtype),
            scratch_shapes=[pltpu.SemaphoreType.DMA((bins,))],
            input_output_aliases={1: 0},
        )(*near(block), *far(fitted))
        finals, fitted = gather(final, n_orig, fitted)
        gap = pl.pallas_call(
            gap_kernel,
            compiler_params=LIMIT,
            in_specs=[whole(pltpu.SMEM), whole(), whole()] + [whole()] * len(finals),
            out_specs=whole(),
            out_shape=jax.ShapeDtypeStruct((bins, width), F32),
        )(place, *near(span, columns, *finals))
        return fitted, gap

    return on_device


def solution(mesh):
    placed = (
        P("tm", "orig", None, None),
        P("tm", "orig"),
        P("tm", None),
        P("orig", None, None),
        P("orig"),
    )
    return jax.shard_map(
        make(mesh),
        mesh=mesh,
        in_specs=placed,
        out_specs=(P("tm", "orig", None, None), P("tm", "orig")),
        check_vma=False,
    )
```

time: 87 us -> 81.1 us (0.932)
  waiting for transfers between devices: 28.3 us -> 16 us
  starting transfers between devices: 40.4 us -> 46 us
  other arithmetic: 0.22 us -> 1.31 us
    ppermute x6, waiting for transfers between devices: 14.6 us -> 4.9 us  [over_first(): return lax.ppermute(x, 'tm', [(i, i ^ 2) for i in range(4)])]
    ppermute x8, starting transfers between devices: 26.1 us -> 32.6 us  [swap(): return lax.ppermute(y, 'orig', [(i, i ^ k) for i in range(n)])]
    ppermute x6, starting transfers between devices: 9.08 us -> 5.03 us  [over_second(): return lax.ppermute(x, 'tm', [(i, i ^ 1) for i in range(4)])]
    ppermute x8, waiting for transfers between devices: 13.3 us -> 9.32 us  [swap(): return lax.ppermute(y, 'orig', [(i, i ^ k) for i in range(n)])]
    ppermute x6, starting transfers between devices: 5.17 us -> 8.35 us  [over_first(): return lax.ppermute(x, 'tm', [(i, i ^ 2) for i in range(4)])]
    ppermute x6, waiting for transfers between devices: 0.45 us -> 1.73 us  [over_second(): return lax.ppermute(x, 'tm', [(i, i ^ 1) for i in range(4)])]
    div x0 -> x2, other arithmetic: none -> 1.02 us  [factor(): return wanted[2 * r + k] / (mine + other + empty)]
    pallas_call x7, Pallas kernels: 7.54 us -> 8.43 us  [the longest x1 2.05 us: cycle(): pl.pallas_call(functools.partial(rest_kernel, start=ranges[r][0], ready_s...]
  transfers between devices with their start and end apart: 20 -> 20, of which waited for: 11 -> 12; matrix products, arithmetic and copies ran while one was open for 0% -> 1% of each run, Pallas kernels for 6% -> 9%
where the time goes in v1:
time: 81.1 us; the launch traced here: 80.9 us
  starting transfers between devices  46 us (57%)
  waiting for transfers between devices  16 us (20%)
  Pallas kernels  15.7 us (19%)
  between operations  1.38 us (2%)
  other arithmetic  1.31 us (2%)
    ppermute x8, starting transfers between devices, swap(): return lax.ppermute(y, 'orig', [(i, i ^ k) for i in range(n)])  32.6 us
    ppermute x8, waiting for transfers between devices, swap(): return lax.ppermute(y, 'orig', [(i, i ^ k) for i in range(n)])  9.32 us
    ppermute x6, starting transfers between devices, over_first(): return lax.ppermute(x, 'tm', [(i, i ^ 2) for i in range(4)])  8.35 us
    ppermute x6, starting transfers between devices, over_second(): return lax.ppermute(x, 'tm', [(i, i ^ 1) for i in range(4)])  5.03 us
    ppermute x6, waiting for transfers between devices, over_first(): return lax.ppermute(x, 'tm', [(i, i ^ 2) for i in range(4)])  4.9 us
    pallas_call x1, Pallas kernels, on_device(): pl.pallas_call(functools.partial(anchor_kernel, starts=cuts[:-1]), compil...  4.26 us
    pallas_call x1, Pallas kernels, cycle(): pl.pallas_call(functools.partial(rest_kernel, start=ranges[r][0], ready_s...  2.05 us
    ppermute x6, waiting for transfers between devices, over_second(): return lax.ppermute(x, 'tm', [(i, i ^ 1) for i in range(4)])  1.73 us
  transfers between devices with their start and end apart: 20, of which 12 were waited for; matrix products, arithmetic and copies ran while one was open for 1% of the time, Pallas kernels for 9%

profile of v1, /device:TPU:0, one launch (start us, length us, event | category | flops | bytes accessed | tf_op | source)
XLA Modules:
  0.0 80.9 jit_solution(9453919905860364487)
XLA Ops:
  0.7 4.3 %shard_map.68 = (bf16[3,12,256,256]{3,2,1,0:T(8,128)(2,1)S(1)}, f32[3,256,128]{2,1,0:T(8,128)S(1)}, f32[84,128]{1,0:T(8,128)S(1)}, s32[1]{0:T(128)}) custom-call(s32[2]{0:T(128)S(1)} %pad_add_fusion.place, s32[12]{0:T(128)} %cols.1, f32[3,256]{1,0:T(4,128)} %anchor.1, bf16[3,12,256,256]{3,2,1,0:T(8,128)(2,1)} %trips.1), custom_call_target="tpu_custom_call" | custom-call | tf_op jit(solution)/shard_map/pallas_call | solution.py:386
  5.0 5.1 %collective-permute-start.36 = (f32[84,128]{1,0:T(8,128)S(1)}, f32[84,128]{1,0:T(8,128)S(1)}, u32[]{:S(2)}, u32[]{:S(2)}) collective-permute-start(f32[84,128]{1,0:T(8,128)S(1)} %get-tuple-element.189), channel_id=1, source_target_pairs={{0,6},{1,7},{2,4},{3,5},{4,2},{5,3},{6,0},{7,1},{8,14},{9,15},{10,... | collective-permute-start | bytes 129032 | tf_op jit(solution)/shard_map/ppermute | solution.py:363
  12.2 2.9 %collective-permute-done.37 = f32[84,128]{1,0:T(8,128)S(1)} collective-permute-done((f32[84,128]{1,0:T(8,128)S(1)}, f32[84,128]{1,0:T(8,128)S(1)}, u32[]{:S(2)}, u32[]{:S(2)}) %collective-permute-start.37) | collective-permute-done | bytes 43040 | tf_op jit(solution)/shard_map/ppermute | solution.py:363
  16.6 1.5 %shard_map.70 = (f32[6,12,128]{2,1,0:T(8,128)S(1)}, f32[8,12,128]{2,1,0:T(8,128)S(1)}, bf16[3,2,256,256]{3,2,1,0:T(8,128)(2,1)S(1)}, f32[2,64,256]{2,1,0:T(8,128...) custom-call(s32[2]{0:T(128)S(1)} %pad_add_fusion.place, ...), custom_call_target="tpu_custom_call" | custom-call | tf_op jit(solution)/shard_map/pallas_call | solution.py:414
  18.1 27.1 %conditional.1 = (f32[2,64,256]{2,1,0:T(8,128)}, f32[2,64,256]{2,1,0:T(8,128)}, f32[2,64,256]{2,1,0:T(8,128)}, f32[2,64,256]{2,1,0:T(8,128)}, f32[72,128]{1,0:T(8,128)S(1)}, /*index=5*/bf16[3,12,256,256]{3,2,1,0:T(8,128)(2,1)}) conditional(s32[]{:T(128)} %bitcast.6, (s32[2]{0:T(128)S(1)}, bf16[3,12,256,256]{3,2,1,0:T(8,128)(2,1)S(1)}, ...), branch_computations={%region_0.0_spmd, %region_1.0_spmd, %region_2.0_spmd} | conditional | flops 1572888 | bytes 29922196 | solution.py:433
  18.1 1.6 %collective-permute-start.12 = (f32[4,64,256]{2,1,0:T(8,128)S(1)}, f32[4,64,256]{2,1,0:T(8,128)S(1)}, u32[]{:S(2)}, u32[]{:S(2)}) collective-permute-start(f32[4,64,256]{2,1,0:T(8,128)S(1)} %get-tuple-element.104), channel_id=1, source_target_pairs={{0,16},{8,24},{16,0},{24,8},{1,17},{9,25},{17,1},{25,9},{2,18},{10... | collective-permute-start | bytes 786440 | tf_op jit(solution)/shard_map/cond/branch_1_fun/ppermute | solution.py:288
  19.7 1.5 %collective-permute-start.15 = (f32[4,64,256]{2,1,0:T(8,128)S(1)}, f32[4,64,256]{2,1,0:T(8,128)S(1)}, u32[]{:S(2)}, u32[]{:S(2)}) collective-permute-start(f32[4,64,256]{2,1,0:T(8,128)S(1)} %get-tuple-element.107), channel_id=1, source_target_pairs={{0,8},{8,0},{16,24},{24,16},{1,9},{9,1},{17,25},{25,17},{2,10},{10... | collective-permute-start | bytes 786440 | tf_op jit(solution)/shard_map/cond/branch_1_fun/ppermute | solution.py:291
  23.1 2.0 %collective-permute-done.12 = f32[4,64,256]{2,1,0:T(8,128)S(1)} collective-permute-done((f32[4,64,256]{2,1,0:T(8,128)S(1)}, f32[4,64,256]{2,1,0:T(8,128)S(1)}, u32[]{:S(2)}, u32[]{:S(2)}) %collective-permute-start.12) | collective-permute-done | bytes 262176 | tf_op jit(solution)/shard_map/cond/branch_1_fun/ppermute | solution.py:288
  25.2 1.6 %collective-permute-start.13 = (f32[4,64,256]{2,1,0:T(8,128)S(1)}, f32[4,64,256]{2,1,0:T(8,128)S(1)}, u32[]{:S(2)}, u32[]{:S(2)}) collective-permute-start(f32[4,64,256]{2,1,0:T(8,128)S(1)} %add.92), channel_id=1, source_target_pairs={{0,8},{8,0},{16,24},{24,16},{1,9},{9,1},{17,25},{25,17},{2,10},{10... | collective-permute-start | bytes 786440 | tf_op jit(solution)/shard_map/cond/branch_1_fun/ppermute | solution.py:291
  27.1 1.3 %collective-permute-start.16 = (f32[4,64,256]{2,1,0:T(8,128)S(1)}, f32[4,64,256]{2,1,0:T(8,128)S(1)}, u32[]{:S(2)}, u32[]{:S(2)}) collective-permute-start(f32[4,64,256]{2,1,0:T(8,128)S(1)} %add.96), channel_id=1, source_target_pairs={{0,16},{8,24},{16,0},{24,8},{1,17},{9,25},{17,1},{25,9},{2,18},{10... | collective-permute-start | bytes 786440 | tf_op jit(solution)/shard_map/cond/branch_1_fun/ppermute | solution.py:288
  29.2 1.7 %collective-permute-start.9 = (f32[2,64,256]{2,1,0:T(8,128)S(1)}, f32[2,64,256]{2,1,0:T(8,128)S(1)}, u32[]{:S(2)}, u32[]{:S(2)}) collective-permute-start(f32[2,64,256]{2,1,0:T(8,128)S(1)} %add.89), channel_id=1, source_target_pairs={{0,16},{8,24},{16,0},{24,8},{1,17},{9,25},{17,1},{25,9},{2,18},{10... | collective-permute-start | bytes 393224 | tf_op jit(solution)/shard_map/cond/branch_1_fun/ppermute | solution.py:288
  31.0 1.0 %collective-permute-done.13 = f32[4,64,256]{2,1,0:T(8,128)S(1)} collective-permute-done((f32[4,64,256]{2,1,0:T(8,128)S(1)}, f32[4,64,256]{2,1,0:T(8,128)S(1)}, u32[]{:S(2)}, u32[]{:S(2)}) %collective-permute-start.13) | collective-permute-done | bytes 262176 | tf_op jit(solution)/shard_map/cond/branch_1_fun/ppermute | solution.py:291
  32.0 2.9 %collective-permute-done.16 = f32[4,64,256]{2,1,0:T(8,128)S(1)} collective-permute-done((f32[4,64,256]{2,1,0:T(8,128)S(1)}, f32[4,64,256]{2,1,0:T(8,128)S(1)}, u32[]{:S(2)}, u32[]{:S(2)}) %collective-permute-start.16) | collective-permute-done | bytes 262176 | tf_op jit(solution)/shard_map/cond/branch_1_fun/ppermute | solution.py:288
  35.1 1.3 %collective-permute-start.14 = (f32[4,64,256]{2,1,0:T(8,128)S(1)}, f32[4,64,256]{2,1,0:T(8,128)S(1)}, u32[]{:S(2)}, u32[]{:S(2)}) collective-permute-start(f32[4,64,256]{2,1,0:T(8,128)S(1)} %get-tuple-element.227.refs_0_), channel_id=1, source_target_pairs={{0,16},{8,24},{16,0},{24,8},{1,17},{9,25},{17,1},{25,9},{2,18},{10... | collective-permute-start | bytes 786440 | tf_op jit(solution)/shard_map/cond/branch_1_fun/ppermute | solution.py:288
  37.5 1.9 %collective-permute-start.10 = (f32[2,64,256]{2,1,0:T(8,128)}, f32[2,64,256]{2,1,0:T(8,128)}, u32[]{:S(2)}, u32[]{:S(2)}) collective-permute-start(f32[2,64,256]{2,1,0:T(8,128)} %get-tuple-element.242), channel_id=1, source_target_pairs={{0,16},{8,24},{16,0},{24,8},{1,17},{9,25},{17,1},{25,9},{2,18},{10... | collective-permute-start | bytes 393224 | tf_op jit(solution)/shard_map/cond/branch_1_fun/ppermute | solution.py:288
  40.0 1.5 %branch_1_fun.5 = (f32[72,128]{1,0:T(8,128)S(1)}, bf16[3,12,256,256]{3,2,1,0:T(8,128)(2,1)}) custom-call(), custom_call_target="tpu_custom_call" | custom-call | tf_op jit(solution)/shard_map/cond/branch_1_fun/pallas_call | solution.py:319
  41.6 1.0 %branch_1_fun.6 = (bf16[3,4,256,256]{3,2,1,0:T(8,128)(2,1)S(1)}, f32[72,128]{1,0:T(8,128)S(1)}) custom-call(s32[2]{0:T(128)S(1)} %get-tuple-element.92.place, bf16[3,12,256,256]{3,2,1,0:T(8,128)(2,1)S(1)} %get-tuple-element.93.trips, f32[3,256,128]{2,1,0:T(8,128)S(1)} %get-tuple-element.94.acol, f32[6,12,128]{2,1,0:T(8,128)S(1)} %get-tuple-element.95.gain, ...), custom_call_target="tpu_custom_call" | custom-call | tf_op jit(solution)/shard_map/cond/branch_1_fun/pallas_call | solution.py:327
  42.8 2.0 %branch_1_fun.7 = (bf16[3,4,256,256]{3,2,1,0:T(8,128)(2,1)S(1)}, f32[72,128]{1,0:T(8,128)S(1)}, bf16[3,12,256,256]{3,2,1,0:T(8,128)(2,1)}) custom-call(s32[2]{0:T(128)S(1)} %get-tuple-element.92.place, bf16[3,12,256,256]{3,2,1,0:T(8,128)(2,1)S(1)} %get-tuple-element.93.trips, ...), custom_call_target="tpu_custom_call", output_to_operand_aliasing={{0}: (7, {}), {2}: (8, {})} | custom-call | tf_op jit(solution)/shard_map/cond/branch_1_fun/pallas_call | solution.py:340
  45.3 1.5 %shard_map.71 = (bf16[3,2,256,256]{3,2,1,0:T(8,128)(2,1)S(1)}, f32[72,128]{1,0:T(8,128)S(1)}) custom-call(s32[2]{0:T(128)S(1)} %pad_add_fusion.place, bf16[3,2,256,256]{3,2,1,0:T(8,128)(2,1)S(1)} %get-tuple-element.195.trips, f32[3,256,128]{2,1,0:T(8,128)S(1)} %get-tuple-element.188.acol, f32[6,12,128]{2,1,0:T(8,128)S(1)} %get-tuple-element.196.gain, ...), custom_call_target="tpu_custom_call" | custom-call | tf_op jit(solution)/shard_map/pallas_call | solution.py:444
  46.7 25.9 %collective-permute-start.40 = (f32[72,128]{1,0:T(8,128)S(1)}, f32[72,128]{1,0:T(8,128)S(1)}, u32[]{:S(2)}, u32[]{:S(2)}) collective-permute-start(f32[72,128]{1,0:T(8,128)S(1)} %get-tuple-element.215), channel_id=1, source_target_pairs={{0,6},{1,7},{2,4},{3,5},{4,2},{5,3},{6,0},{7,1},{8,14},{9,15},{10,... | collective-permute-start | bytes 110600 | tf_op jit(solution)/shard_map/ppermute | solution.py:363
  73.4 0.9 %shard_map.72 = bf16[3,12,256,256]{3,2,1,0:T(8,128)(2,1)} custom-call(bf16[3,2,256,256]{3,2,1,0:T(8,128)(2,1)S(1)} %get-tuple-element.216.local, bf16[3,12,256,256]{3,2,1,0:T(8,128)(2,1)} %get-tuple-element.217.before), custom_call_target="tpu_custom_call", output_to_operand_aliasing={{}: (1, {})} | custom-call | tf_op jit(solution)/shard_map/pallas_call | solution.py:454
  74.6 3.3 %collective-permute-done.41 = f32[72,128]{1,0:T(8,128)S(1)} collective-permute-done((f32[72,128]{1,0:T(8,128)S(1)}, f32[72,128]{1,0:T(8,128)S(1)}, u32[]{:S(2)}, u32[]{:S(2)}) %collective-permute-start.41) | collective-permute-done | bytes 36896 | tf_op jit(solution)/shard_map/ppermute | solution.py:363
  78.0 1.4 %collective-permute-done.43.refs_2_ = f32[4,72,128]{2,1,0:T(8,128)S(1)} collective-permute-done((f32[4,72,128]{2,1,0:T(8,128)S(1)}, f32[4,72,128]{2,1,0:T(8,128)S(1)}, u32[]{:S(2)}, u32[]{:S(2)}) %collective-permute-start.43) | collective-permute-done | bytes 147488 | tf_op jit(solution)/shard_map/ppermute | solution.py:363
  79.4 1.5 %shard_map.73 = f32[3,4096]{1,0:T(4,128)} custom-call(s32[2]{0:T(128)S(1)} %pad_add_fusion.place, f32[3,4096]{1,0:T(4,128)S(1)} %get-tuple-element.219.span, f32[8,12,128]{2,1,0:T(8,128)S(1)} %get-tuple-element.220.refs_0_, f32[4,72,128]{2,1,0:T(8,128)S(1)} %pad_maximum_fusion.1.refs_1_, f32[4,72,128]{2,1,0:T(8,128)S(1)} %collective-permute-done.43.refs_2_), custom_call_target="tpu_custom_call" | custom-call | tf_op jit(solution)/shard_map/pallas_call | solution.py:464
  (44 shorter events, 9.3 us)
Async XLA Ops:
  0.6 10.2 %copy-start.2 = (s32[12]{0:T(128)S(1)}, s32[12]{0:T(128)}, u32[]{:S(2)}) copy-start(s32[12]{0:T(128)} %cols.1) | copy-start | bytes 148
  0.6 10.2 %copy-start.1 = (f32[3,32768]{1,0:T(4,128)S(1)}, f32[3,32768]{1,0:T(4,128)}, u32[]{:S(2)}) copy-start(f32[3,32768]{1,0:T(4,128)} %dest.1) | copy-start | bytes 1179652
  0.7 10.2 %copy-start = (bf16[12,256,256]{2,1,0:T(8,128)(2,1)S(1)}, bf16[12,256,256]{2,1,0:T(8,128)(2,1)}, u32[]{:S(2)}) copy-start(bf16[12,256,256]{2,1,0:T(8,128)(2,1)} %target.1) | copy-start | bytes 4718596
  5.0 7.2 %collective-permute-start.36 = (f32[84,128]{1,0:T(8,128)S(1)}, f32[84,128]{1,0:T(8,128)S(1)}, u32[]{:S(2)}, u32[]{:S(2)}) collective-permute-start(f32[84,128]{1,0:T(8,128)S(1)} %get-tuple-element.189), channel_id=1, source_target_pairs={{0,6},{1,7},{2,4},{3,5},{4,2},{5,3},{6,0},{7,1},{8,14},{9,15},{10,... | collective-permute-start | bytes 129032 | tf_op jit(solution)/shard_map/ppermute | solution.py:363
  10.2 4.9 %collective-permute-start.37 = (f32[84,128]{1,0:T(8,128)S(1)}, f32[84,128]{1,0:T(8,128)S(1)}, u32[]{:S(2)}, u32[]{:S(2)}) collective-permute-start(f32[84,128]{1,0:T(8,128)S(1)} %get-tuple-element.189), channel_id=1, source_target_pairs={{0,4},{1,5},{2,6},{3,7},{4,0},{5,1},{6,2},{7,3},{8,12},{9,13},{10,... | collective-permute-start | bytes 129032 | tf_op jit(solution)/shard_map/ppermute | solution.py:363
  10.2 4.9 %collective-permute-start.38 = (f32[84,128]{1,0:T(8,128)S(1)}, f32[84,128]{1,0:T(8,128)S(1)}, u32[]{:S(2)}, u32[]{:S(2)}) collective-permute-start(f32[84,128]{1,0:T(8,128)S(1)} %get-tuple-element.189), channel_id=1, source_target_pairs={{0,2},{1,3},{2,0},{3,1},{4,6},{5,7},{6,4},{7,5},{8,10},{9,11},{10,... | collective-permute-start | bytes 129032 | tf_op jit(solution)/shard_map/ppermute | solution.py:363
  15.1 1.5 %collective-permute-start.39 = (f32[4,84,128]{2,1,0:T(8,128)S(1)}, f32[4,84,128]{2,1,0:T(8,128)S(1)}, u32[]{:S(2)}, u32[]{:S(2)}) collective-permute-start(f32[4,84,128]{2,1,0:T(8,128)S(1)} %pad_maximum_fusion.refs_0_), channel_id=1, source_target_pairs={{0,1},{1,0},{2,3},{3,2},{4,5},{5,4},{6,7},{7,6},{8,9},{9,8},{10,11... | collective-permute-start | bytes 516104 | tf_op jit(solution)/shard_map/ppermute | solution.py:363
  18.1 7.0 %collective-permute-start.12 = (f32[4,64,256]{2,1,0:T(8,128)S(1)}, f32[4,64,256]{2,1,0:T(8,128)S(1)}, u32[]{:S(2)}, u32[]{:S(2)}) collective-permute-start(f32[4,64,256]{2,1,0:T(8,128)S(1)} %get-tuple-element.104), channel_id=1, source_target_pairs={{0,16},{8,24},{16,0},{24,8},{1,17},{9,25},{17,1},{25,9},{2,18},{10... | collective-permute-start | bytes 786440 | tf_op jit(solution)/shard_map/cond/branch_1_fun/ppermute | solution.py:288
  19.7 7.3 %collective-permute-start.15 = (f32[4,64,256]{2,1,0:T(8,128)S(1)}, f32[4,64,256]{2,1,0:T(8,128)S(1)}, u32[]{:S(2)}, u32[]{:S(2)}) collective-permute-start(f32[4,64,256]{2,1,0:T(8,128)S(1)} %get-tuple-element.107), channel_id=1, source_target_pairs={{0,8},{8,0},{16,24},{24,16},{1,9},{9,1},{17,25},{25,17},{2,10},{10... | collective-permute-start | bytes 786440 | tf_op jit(solution)/shard_map/cond/branch_1_fun/ppermute | solution.py:291
  21.2 7.2 %collective-permute-start.6 = (f32[2,64,256]{2,1,0:T(8,128)S(1)}, f32[2,64,256]{2,1,0:T(8,128)S(1)}, u32[]{:S(2)}, u32[]{:S(2)}) collective-permute-start(f32[2,64,256]{2,1,0:T(8,128)S(1)} %get-tuple-element.97), channel_id=1, source_target_pairs={{0,16},{8,24},{16,0},{24,8},{1,17},{9,25},{17,1},{25,9},{2,18},{10... | collective-permute-start | bytes 393224 | tf_op jit(solution)/shard_map/cond/branch_1_fun/ppermute | solution.py:288
  21.7 7.5 %collective-permute-start.8 = (f32[2,64,256]{2,1,0:T(8,128)S(1)}, f32[2,64,256]{2,1,0:T(8,128)S(1)}, u32[]{:S(2)}, u32[]{:S(2)}) collective-permute-start(f32[2,64,256]{2,1,0:T(8,128)S(1)} %get-tuple-element.101), channel_id=1, source_target_pairs={{0,8},{8,0},{16,24},{24,16},{1,9},{9,1},{17,25},{25,17},{2,10},{10... | collective-permute-start | bytes 393224 | tf_op jit(solution)/shard_map/cond/branch_1_fun/ppermute | solution.py:291
  25.2 6.8 %collective-permute-start.13 = (f32[4,64,256]{2,1,0:T(8,128)S(1)}, f32[4,64,256]{2,1,0:T(8,128)S(1)}, u32[]{:S(2)}, u32[]{:S(2)}) collective-permute-start(f32[4,64,256]{2,1,0:T(8,128)S(1)} %add.92), channel_id=1, source_target_pairs={{0,8},{8,0},{16,24},{24,16},{1,9},{9,1},{17,25},{25,17},{2,10},{10... | collective-permute-start | bytes 786440 | tf_op jit(solution)/shard_map/cond/branch_1_fun/ppermute | solution.py:291
  27.1 7.7 %collective-permute-start.16 = (f32[4,64,256]{2,1,0:T(8,128)S(1)}, f32[4,64,256]{2,1,0:T(8,128)S(1)}, u32[]{:S(2)}, u32[]{:S(2)}) collective-permute-start(f32[4,64,256]{2,1,0:T(8,128)S(1)} %add.96), channel_id=1, source_target_pairs={{0,16},{8,24},{16,0},{24,8},{1,17},{9,25},{17,1},{25,9},{2,18},{10... | collective-permute-start | bytes 786440 | tf_op jit(solution)/shard_map/cond/branch_1_fun/ppermute | solution.py:288
  28.5 8.2 %collective-permute-start.7 = (f32[2,64,256]{2,1,0:T(8,128)S(1)}, f32[2,64,256]{2,1,0:T(8,128)S(1)}, u32[]{:S(2)}, u32[]{:S(2)}) collective-permute-start(f32[2,64,256]{2,1,0:T(8,128)S(1)} %add.85), channel_id=1, source_target_pairs={{0,8},{8,0},{16,24},{24,16},{1,9},{9,1},{17,25},{25,17},{2,10},{10... | collective-permute-start | bytes 393224 | tf_op jit(solution)/shard_map/cond/branch_1_fun/ppermute | solution.py:291
  29.2 7.5 %collective-permute-start.9 = (f32[2,64,256]{2,1,0:T(8,128)S(1)}, f32[2,64,256]{2,1,0:T(8,128)S(1)}, u32[]{:S(2)}, u32[]{:S(2)}) collective-permute-start(f32[2,64,256]{2,1,0:T(8,128)S(1)} %add.89), channel_id=1, source_target_pairs={{0,16},{8,24},{16,0},{24,8},{1,17},{9,25},{17,1},{25,9},{2,18},{10... | collective-permute-start | bytes 393224 | tf_op jit(solution)/shard_map/cond/branch_1_fun/ppermute | solution.py:288
  35.1 7.5 %collective-permute-start.14 = (f32[4,64,256]{2,1,0:T(8,128)S(1)}, f32[4,64,256]{2,1,0:T(8,128)S(1)}, u32[]{:S(2)}, u32[]{:S(2)}) collective-permute-start(f32[4,64,256]{2,1,0:T(8,128)S(1)} %get-tuple-element.227.refs_0_), channel_id=1, source_target_pairs={{0,16},{8,24},{16,0},{24,8},{1,17},{9,25},{17,1},{25,9},{2,18},{10... | collective-permute-start | bytes 786440 | tf_op jit(solution)/shard_map/cond/branch_1_fun/ppermute | solution.py:288
  36.4 6.4 %collective-permute-start.17 = (f32[4,64,256]{2,1,0:T(8,128)S(1)}, f32[4,64,256]{2,1,0:T(8,128)S(1)}, u32[]{:S(2)}, u32[]{:S(2)}) collective-permute-start(f32[4,64,256]{2,1,0:T(8,128)S(1)} %get-tuple-element.226.refs_1_), channel_id=1, source_target_pairs={{0,8},{8,0},{16,24},{24,16},{1,9},{9,1},{17,25},{25,17},{2,10},{10... | collective-permute-start | bytes 786440 | tf_op jit(solution)/shard_map/cond/branch_1_fun/ppermute | solution.py:291
  37.5 7.3 %collective-permute-start.10 = (f32[2,64,256]{2,1,0:T(8,128)}, f32[2,64,256]{2,1,0:T(8,128)}, u32[]{:S(2)}, u32[]{:S(2)}) collective-permute-start(f32[2,64,256]{2,1,0:T(8,128)} %get-tuple-element.242), channel_id=1, source_target_pairs={{0,16},{8,24},{16,0},{24,8},{1,17},{9,25},{17,1},{25,9},{2,18},{10... | collective-permute-start | bytes 393224 | tf_op jit(solution)/shard_map/cond/branch_1_fun/ppermute | solution.py:288
  39.5 5.3 %collective-permute-start.11 = (f32[2,64,256]{2,1,0:T(8,128)}, f32[2,64,256]{2,1,0:T(8,128)}, u32[]{:S(2)}, u32[]{:S(2)}) collective-permute-start(f32[2,64,256]{2,1,0:T(8,128)} %get-tuple-element.243), channel_id=1, source_target_pairs={{0,8},{8,0},{16,24},{24,16},{1,9},{9,1},{17,25},{25,17},{2,10},{10... | collective-permute-start | bytes 393224 | tf_op jit(solution)/shard_map/cond/branch_1_fun/ppermute | solution.py:291
  46.7 27.9 %collective-permute-start.40 = (f32[72,128]{1,0:T(8,128)S(1)}, f32[72,128]{1,0:T(8,128)S(1)}, u32[]{:S(2)}, u32[]{:S(2)}) collective-permute-start(f32[72,128]{1,0:T(8,128)S(1)} %get-tuple-element.215), channel_id=1, source_target_pairs={{0,6},{1,7},{2,4},{3,5},{4,2},{5,3},{6,0},{7,1},{8,14},{9,15},{10,... | collective-permute-start | bytes 110600 | tf_op jit(solution)/shard_map/ppermute | solution.py:363
  72.6 5.3 %collective-permute-start.41 = (f32[72,128]{1,0:T(8,128)S(1)}, f32[72,128]{1,0:T(8,128)S(1)}, u32[]{:S(2)}, u32[]{:S(2)}) collective-permute-start(f32[72,128]{1,0:T(8,128)S(1)} %get-tuple-element.215), channel_id=1, source_target_pairs={{0,4},{1,5},{2,6},{3,7},{4,0},{5,1},{6,2},{7,3},{8,12},{9,13},{10,... | collective-permute-start | bytes 110600 | tf_op jit(solution)/shard_map/ppermute | solution.py:363
  72.9 5.0 %collective-permute-start.42 = (f32[72,128]{1,0:T(8,128)S(1)}, f32[72,128]{1,0:T(8,128)S(1)}, u32[]{:S(2)}, u32[]{:S(2)}) collective-permute-start(f32[72,128]{1,0:T(8,128)S(1)} %get-tuple-element.215), channel_id=1, source_target_pairs={{0,2},{1,3},{2,0},{3,1},{4,6},{5,7},{6,4},{7,5},{8,10},{9,11},{10,... | collective-permute-start | bytes 110600 | tf_op jit(solution)/shard_map/ppermute | solution.py:363
  77.9 1.4 %collective-permute-start.43 = (f32[4,72,128]{2,1,0:T(8,128)S(1)}, f32[4,72,128]{2,1,0:T(8,128)S(1)}, u32[]{:S(2)}, u32[]{:S(2)}) collective-permute-start(f32[4,72,128]{2,1,0:T(8,128)S(1)} %pad_maximum_fusion.1.refs_1_), channel_id=1, source_target_pairs={{0,1},{1,0},{2,3},{3,2},{4,5},{5,4},{6,7},{7,6},{8,9},{9,8},{10,11... | collective-permute-start | bytes 442376 | tf_op jit(solution)/shard_map/ppermute | solution.py:363

commit v2 on v1

--- a/solution.py
+++ b/solution.py
@@ -148,8 +148,7 @@
 
 
 def day_kernel(place, trips, acol, picked, *refs, ranges, count):
-    arrived, gain, columns, first_trips, outs = refs[:count], refs[count], refs[count + 1], refs[count + 2], refs[count + 3 :]
-    first_trips[...] = trips[:, : first_trips.shape[1]]
+    arrived, gain, columns, outs = refs[:count], refs[count], refs[count + 1], refs[count + 2 :]
     bins, slots, side, _ = trips.shape
     halves = side // LANES
     parts = bins * halves
@@ -244,31 +243,33 @@
         fit_rows(place, trips, acol, gain, factors[2 * r], factors[2 * r + 1], locals_[r], sums, start, True)
 
 
-def rest_kernel(place, trips, acol, gain, fa, fb, sums_in, mine, *refs, start, ready_start, chained, last):
-    refs = list(refs)
-    ready = refs.pop(0) if ready_start is not None else None
-    if chained:
-        refs.pop(0)
-    local, sums = refs[:2]
-    bins, count, _, _ = local.shape
-    copies = []
-    if ready is not None:
-        fitted, done = refs[2:]
-        pairs = [(ready.at[t], fitted.at[t, ready_start : ready_start + ready.shape[1]]) for t in range(bins)]
-        copies += copy_all(pairs, done)
+def rest_kernel(place, trips, acol, gain, fa, fb, sums_in, mine, local, sums, *refs, start):
     sums[...] = sums_in[...]
     fit_rows(place, trips, acol, gain, fa, fb, local, sums, start, False)
-    if last:
-        fitted, done = refs[2:]
-        copies += copy_all([(local.at[t], fitted.at[t, start : start + count]) for t in range(bins)], done, len(copies))
-    for copy in copies:
-        copy.wait()
-
-
-def end_kernel(place, trips, acol, gain, fa, fb, ga, gb, sums_in, local, sums, *, start):
+    if refs:
+        fitted, done = refs
+        bins, count, _, _ = local.shape
+        for copy in copy_all([(local.at[t], fitted.at[t, start : start + count]) for t in range(bins)], done):
+            copy.wait()
+
+
+def end_kernel(place, trips, acol, gain, fa, fb, ga, gb, sums_in, *refs, start, ready_start, chained):
+    refs = list(refs)
+    copies = []
+    if ready_start is None:
+        local, sums = refs
+    else:
+        ready = refs.pop(0)
+        if chained:
+            refs.pop(0)
+        local, sums, fitted, done = refs
+        bins, count, _, _ = ready.shape
+        copies = copy_all([(ready.at[t], fitted.at[t, ready_start : ready_start + count]) for t in range(bins)], done)
     sums[...] = sums_in[...]
     fit_rows(place, trips, acol, gain, fa, fb, local, sums, start, True)
     fit_rows(place, trips, acol, gain, ga, gb, local, sums, start, False)
+    for copy in copies:
+        copy.wait()
 
 
 def store_kernel(local, before, fitted, done, *, start):
@@ -277,7 +278,10 @@
         copy.wait()
 
 
-def cycle(trips, acol, gain, cols, place, wanted, sends, *, ranges, used):
+def cycle(trips, acol, gain, cols, place, wanted, sends, *, ranges):
+    used = len(ranges)
+    wanted = [wanted[2 * r + k][: ranges[r][1]] for r in range(used) for k in range(2)]
+    sends = [sends[2 * r + k][: ranges[r][1]] for r in range(used) for k in range(2)]
     bins, slots, side, _ = trips.shape
     halves = side // LANES
     rows = side // 4
@@ -300,11 +304,11 @@
 
     got = {r: (over_first(sends[2 * r]), over_second(sends[2 * r + 1])) for r in order}
     kept = pl.pallas_call(
-        functools.partial(keep_kernel, ranges=ranges[:used]),
+        functools.partial(keep_kernel, ranges=ranges),
         compiler_params=LIMIT,
         in_specs=[whole(pltpu.SMEM)] + [whole()] * 3,
         out_specs=[whole()] * (2 * used),
-        out_shape=[pltpu.VMEM((n, rows, side), F32) for _, n in ranges[:used] for _ in range(2)],
+        out_shape=[pltpu.VMEM((n, rows, side), F32) for _, n in ranges for _ in range(2)],
     )(place, *near(trips, acol, gain))
     mine = {r: [total(kept[2 * r + k], got[r][k]) for k in range(2)] for r in order}
     other = {r: (over_second(mine[r][0]), over_first(mine[r][1])) for r in order}
@@ -314,8 +318,8 @@
     final = pltpu.VMEM((parts * slots, LANES), F32)
     store = pltpu.HBM(trips.shape, trips.dtype)
     sums, fitted = jnp.zeros((parts * slots, LANES), F32), None
-    if used < len(ranges):
-        empty = range(ranges[used][0], slots)
+    empty = range(sum(count for _, count in ranges), slots)
+    if empty:
         sums, fitted = pl.pallas_call(
             functools.partial(empty_kernel, empty=empty),
             compiler_params=LIMIT,
@@ -325,37 +329,42 @@
         )()
     if used > 1:
         *out, sums = pl.pallas_call(
-            functools.partial(kept_kernel, ranges=ranges[1:used]),
+            functools.partial(kept_kernel, ranges=ranges[1:]),
             compiler_params=LIMIT,
             in_specs=[whole(pltpu.SMEM)] + [whole()] * (4 + 2 * (used - 1)),
             out_specs=[whole()] * used,
             out_shape=[*shapes[1:used], final],
         )(place, *near(trips, acol, gain, sums, *[f for r in range(1, used) for f in scale[r]]))
         out = [None] + out
+    else:
+        out = [None]
     for r in order[:-1]:
-        ready = [out[r + 1]] if r + 1 < used else []
-        last = r == 1
-        writes = len(ready) + last
-        chain = far(fitted) if writes and fitted is not None else []
+        leaves = r > 1
         outs = pl.pallas_call(
-            functools.partial(
-                rest_kernel,
-                start=ranges[r][0],
-                ready_start=ranges[r + 1][0] if ready else None,
-                chained=len(chain) > 0,
-                last=last,
-            ),
-            compiler_params=LIMIT,
-            in_specs=[whole(pltpu.SMEM)] + [whole()] * (7 + len(ready)) + [whole(pltpu.HBM)] * len(chain),
-            out_specs=[whole(), whole()] + [whole(pltpu.HBM)] * (writes > 0),
-            out_shape=[shapes[r], final] + [store] * (writes > 0),
-            scratch_shapes=[pltpu.SemaphoreType.DMA((bins * writes,))] * (writes > 0),
-            input_output_aliases={7: 0} | ({8 + len(ready): 2} if chain else {}),
-        )(place, *near(trips, acol, gain, *back[r], sums, out[r], *ready), *chain)
+            functools.partial(rest_kernel, start=ranges[r][0]),
+            compiler_params=LIMIT,
+            in_specs=[whole(pltpu.SMEM)] + [whole()] * 7,
+            out_specs=[whole(), whole()] + [whole(pltpu.HBM)] * leaves,
+            out_shape=[shapes[r], final] + [store] * leaves,
+            scratch_shapes=[pltpu.SemaphoreType.DMA((bins,))] * leaves,
+            input_output_aliases={7: 0},
+        )(place, *near(trips, acol, gain, *back[r], sums, out[r]))
         out[r], sums = outs[:2]
-        if writes:
+        if leaves:
             fitted = outs[2]
-    return [*scale[0], *back[0]], sums, fitted
+    ready = [out[1]] if used > 1 else []
+    outs = pl.pallas_call(
+        functools.partial(
+            end_kernel, start=ranges[0][0], ready_start=ranges[1][0] if ready else None, chained=len(ready) > 0
+        ),
+        compiler_params=LIMIT,
+        in_specs=[whole(pltpu.SMEM)] + [whole()] * (8 + len(ready)) + [whole(pltpu.HBM)] * len(ready),
+        out_specs=[whole(), whole()] + [whole(pltpu.HBM)] * len(ready),
+        out_shape=[shapes[0], final] + [store] * len(ready),
+        scratch_shapes=[pltpu.SemaphoreType.DMA((bins,))] * len(ready),
+        input_output_aliases={10: 2} if ready else {},
+    )(place, *near(trips, acol, gain, *scale[0], *back[0], sums, *ready), *(far(fitted) if ready else []))
+    return outs[2] if ready else fitted, outs[0], outs[1]
 
 
 def gather(x, n, beside):
@@ -381,10 +390,9 @@
         place = jnp.stack([lax.axis_index("tm").astype(jnp.int32), lax.axis_index("orig").astype(jnp.int32)])
         place, block_columns = lax.optimization_barrier((place, block_columns))
 
-        cuts = [max(slots // 6, 1), max(slots // 2, 2), slots]
-        ranges = [(a, b - a) for a, b in zip([0] + cuts, cuts)]
+        ranges, plans = plans_of(slots)
         local, acol, sums, pick = pl.pallas_call(
-            functools.partial(anchor_kernel, starts=cuts[:-1]),
+            functools.partial(anchor_kernel, starts=[sum(n for _, n in plan) for plan in plans[:-1]]),
             compiler_params=LIMIT,
             in_specs=[whole(pltpu.SMEM), whole(pltpu.SMEM), whole(pltpu.HBM), whole(pltpu.HBM)],
             out_specs=[whole(), whole(), whole(), whole(pltpu.SMEM)],
@@ -411,28 +419,27 @@
         arrived, picked = gather(sums, n_orig, picked)
 
         quarter = side // 4
-        gain, columns, opening, *sends = pl.pallas_call(
+        gain, columns, *sends = pl.pallas_call(
             functools.partial(day_kernel, ranges=ranges, count=len(arrived)),
             compiler_params=LIMIT,
             in_specs=[whole(pltpu.SMEM)] + [whole()] * (3 + len(arrived)),
-            out_specs=[whole()] * (3 + 2 * len(ranges)),
+            out_specs=[whole()] * (2 + 2 * len(ranges)),
             out_shape=[
                 pltpu.VMEM((parts, slots, LANES), F32),
                 pltpu.VMEM((n_orig, slots, LANES), F32),
-                pltpu.VMEM((bins, ranges[0][1], side, side), trip_counts.dtype),
             ]
             + [pltpu.VMEM((n, quarter, side), F32) for _, n in ranges for _ in range(2)],
         )(place, *near(local, acol, picked, *arrived))
 
         def branch(k):
             def run(*args):
-                return cycle(*args, ranges=ranges, used=k + 1)
+                return cycle(*args, ranges=plans[k])
 
             return run
 
-        factors, final, fitted = lax.switch(
+        fitted, block, final = lax.switch(
             pick[0],
-            [branch(k) for k in range(len(ranges))],
+            [branch(k) for k in range(len(plans))],
             local,
             acol,
             gain,
@@ -441,16 +448,6 @@
             wanted,
             sends,
         )
-        block, final = pl.pallas_call(
-            functools.partial(end_kernel, start=ranges[0][0]),
-            compiler_params=LIMIT,
-            in_specs=[whole(pltpu.SMEM)] + [whole()] * 8,
-            out_specs=[whole(), whole()],
-            out_shape=[
-                pltpu.VMEM((bins, ranges[0][1], side, side), trip_counts.dtype),
-                pltpu.VMEM((parts * slots, LANES), F32),
-            ],
-        )(place, *near(opening, acol, gain, *factors, final))
         fitted = pl.pallas_call(
             functools.partial(store_kernel, start=ranges[0][0]),
             compiler_params=LIMIT,
@@ -473,6 +470,13 @@
     return on_device
 
 
+def plans_of(slots):
+    small, half = max(slots // 6, 1), max(slots // 2, 2)
+    ranges = [(0, small), (small, half - small), (half, slots - half)]
+    plans = [ranges[:1]] + [[ranges[0], (small, n)] for n in range(1, half - small + 1)] + [ranges]
+    return ranges, plans
+
+
 def solution(mesh):
     placed = (
         P("tm", "orig", None, None),
@@ -481,10 +485,11 @@
         P("orig", None, None),
         P("orig"),
     )
-    return jax.shard_map(
+    step = jax.shard_map(
         make(mesh),
         mesh=mesh,
         in_specs=placed,
         out_specs=(P("tm", "orig", None, None), P("tm", "orig")),
         check_vma=False,
     )
+    return lambda *args: step(*args)

time: 81.1 us -> 79.8 us (0.984)
  starting transfers between devices: 46 us -> 48.4 us
  waiting for transfers between devices: 16 us -> 13.7 us
  Pallas kernels: 15.7 us -> 14.2 us
  other arithmetic: 1.31 us -> 0.31 us
    ppermute x6, waiting for transfers between devices: 4.9 us -> 1.73 us  [over_first(): return lax.ppermute(x, 'tm', [(i, i ^ 2) for i in range(4)])]
    pallas_call x5, Pallas kernels: 9.57 us -> 7.57 us  [the longest x1 4.26 us: on_device(): pl.pallas_call(functools.partial(anchor_kernel, starts=[sum((n for _, n i...]
    ppermute x8, starting transfers between devices: 32.6 us -> 34.6 us  [swap(): return lax.ppermute(y, 'orig', [(i, i ^ k) for i in range(n)])]
    ppermute x6, starting transfers between devices: 5.03 us -> 6.27 us  [over_second(): return lax.ppermute(x, 'tm', [(i, i ^ 1) for i in range(4)])]
    ppermute x6, waiting for transfers between devices: 1.73 us -> 2.97 us  [over_second(): return lax.ppermute(x, 'tm', [(i, i ^ 1) for i in range(4)])]
    div x2 -> x3, other arithmetic: 1.02 us -> 0.15 us  [factor(): return wanted[2 * r + k] / (mine + other + empty)]
  transfers between devices with their start and end apart: 20 -> 20, of which waited for: 12 -> 10; matrix products, arithmetic and copies ran while one was open for 1% -> 1% of each run, Pallas kernels for 9% -> 7%
where the time goes in v2:
time: 79.8 us; the launch traced here: 79.6 us
  starting transfers between devices  48.4 us (61%)
  Pallas kernels  14.2 us (18%)
  waiting for transfers between devices  13.7 us (17%)
  between operations  1.37 us (2%)
  loops' own time  1.01 us (1%)
    ppermute x8, starting transfers between devices, swap(): return lax.ppermute(y, 'orig', [(i, i ^ k) for i in range(n)])  34.6 us
    ppermute x8, waiting for transfers between devices, swap(): return lax.ppermute(y, 'orig', [(i, i ^ k) for i in range(n)])  9.03 us
    ppermute x6, starting transfers between devices, over_first(): return lax.ppermute(x, 'tm', [(i, i ^ 2) for i in range(4)])  7.55 us
    ppermute x6, starting transfers between devices, over_second(): return lax.ppermute(x, 'tm', [(i, i ^ 1) for i in range(4)])  6.27 us
    pallas_call x1, Pallas kernels, on_device(): pl.pallas_call(functools.partial(anchor_kernel, starts=[sum((n for _, n i...  4.26 us
    ppermute x6, waiting for transfers between devices, over_second(): return lax.ppermute(x, 'tm', [(i, i ^ 1) for i in range(4)])  2.97 us
    pallas_call x1, Pallas kernels, cycle(): pl.pallas_call(functools.partial(empty_kernel, empty=empty), compiler_par...  2.01 us
    ppermute x6, waiting for transfers between devices, over_first(): return lax.ppermute(x, 'tm', [(i, i ^ 2) for i in range(4)])  1.73 us
  transfers between devices with their start and end apart: 20, of which 10 were waited for; matrix products, arithmetic and copies ran while one was open for 1% of the time, Pallas kernels for 7%

profile of v2, /device:TPU:0, one launch (start us, length us, event | category | flops | bytes accessed | tf_op | source)
XLA Modules:
  0.0 79.6 jit_solution(9437436629527958228)
XLA Ops:
  0.7 4.3 %shard_map.68 = (bf16[3,12,256,256]{3,2,1,0:T(8,128)(2,1)S(1)}, f32[3,256,128]{2,1,0:T(8,128)S(1)}, f32[84,128]{1,0:T(8,128)S(1)}, s32[1]{0:T(128)}) custom-call(s32[2]{0:T(128)S(1)} %pad_add_fusion.place, s32[12]{0:T(128)} %cols.1, f32[3,256]{1,0:T(4,128)} %anchor.1, bf16[3,12,256,256]{3,2,1,0:T(8,128)(2,1)} %trips.1), custom_call_target="tpu_custom_call" | custom-call | tf_op jit(solution)/shard_map/pallas_call | solution.py:394
  5.0 5.1 %collective-permute-start.72 = (f32[84,128]{1,0:T(8,128)S(1)}, f32[84,128]{1,0:T(8,128)S(1)}, u32[]{:S(2)}, u32[]{:S(2)}) collective-permute-start(f32[84,128]{1,0:T(8,128)S(1)} %get-tuple-element.348), channel_id=1, source_target_pairs={{0,6},{1,7},{2,4},{3,5},{4,2},{5,3},{6,0},{7,1},{8,14},{9,15},{10,... | collective-permute-start | bytes 129032 | tf_op jit(solution)/shard_map/ppermute | solution.py:372
  12.2 2.9 %collective-permute-done.73 = f32[84,128]{1,0:T(8,128)S(1)} collective-permute-done((f32[84,128]{1,0:T(8,128)S(1)}, f32[84,128]{1,0:T(8,128)S(1)}, u32[]{:S(2)}, u32[]{:S(2)}) %collective-permute-start.73) | collective-permute-done | bytes 43040 | tf_op jit(solution)/shard_map/ppermute | solution.py:372
  15.9 0.8 collective-permute-done.75.refs_1_
  16.6 1.5 %shard_map.70 = (f32[6,12,128]{2,1,0:T(8,128)S(1)}, f32[8,12,128]{2,1,0:T(8,128)S(1)}, f32[2,64,256]{2,1,0:T(8,128)S(1)}, f32[2,64,256]{2,1,0:T(8,128)S(1)}, f32...) custom-call(s32[2]{0:T(128)S(1)} %pad_add_fusion.place, ...), custom_call_target="tpu_custom_call" | custom-call | tf_op jit(solution)/shard_map/pallas_call | solution.py:422
  18.1 25.7 %conditional.1 = (bf16[3,12,256,256]{3,2,1,0:T(8,128)(2,1)}, bf16[3,2,256,256]{3,2,1,0:T(8,128)(2,1)S(1)}, f32[72,128]{1,0:T(8,128)S(1)}) conditional(s32[]{:T(128)} %bitcast.3, (s32[2]{0:T(128)S(1)}, bf16[3,12,256,256]{3,2,1,0:T(8,128)(2,1)S(1)}, f32[3,256,128]{2,1,0:T(8,128)S(1)}, f32[6,12,128]{2,1,0:T(8,128)S(1)}, ...), branch_computations={%region_0.0_spmd, %region_1.0_spmd, %region_2.0_spmd, %region_3.0_... | conditional | flops 1572888 | bytes 29922172 | solution.py:440
  18.1 1.6 %collective-permute-start.12 = (f32[1,64,256]{2,1,0:T(8,128)S(1)}, f32[1,64,256]{2,1,0:T(8,128)S(1)}, u32[]{:S(2)}, u32[]{:S(2)}) collective-permute-start(f32[1,64,256]{2,1,0:T(8,128)S(1)} %slice.53), channel_id=1, source_target_pairs={{0,16},{8,24},{16,0},{24,8},{1,17},{9,25},{17,1},{25,9},{2,18},{10... | collective-permute-start | bytes 196616 | tf_op jit(solution)/shard_map/cond/branch_1_fun/ppermute | solution.py:292
  19.7 1.5 %collective-permute-start.15 = (f32[1,64,256]{2,1,0:T(8,128)S(1)}, f32[1,64,256]{2,1,0:T(8,128)S(1)}, u32[]{:S(2)}, u32[]{:S(2)}) collective-permute-start(f32[1,64,256]{2,1,0:T(8,128)S(1)} %slice.60), channel_id=1, source_target_pairs={{0,8},{8,0},{16,24},{24,16},{1,9},{9,1},{17,25},{25,17},{2,10},{10... | collective-permute-start | bytes 196616 | tf_op jit(solution)/shard_map/cond/branch_1_fun/ppermute | solution.py:295
  23.0 1.6 %collective-permute-start.13 = (f32[1,64,256]{2,1,0:T(8,128)S(1)}, f32[1,64,256]{2,1,0:T(8,128)S(1)}, u32[]{:S(2)}, u32[]{:S(2)}) collective-permute-start(f32[1,64,256]{2,1,0:T(8,128)S(1)} %add.184), channel_id=1, source_target_pairs={{0,8},{8,0},{16,24},{24,16},{1,9},{9,1},{17,25},{25,17},{2,10},{10... | collective-permute-start | bytes 196616 | tf_op jit(solution)/shard_map/cond/branch_1_fun/ppermute | solution.py:295
  25.8 1.6 %collective-permute-start.16 = (f32[1,64,256]{2,1,0:T(8,128)S(1)}, f32[1,64,256]{2,1,0:T(8,128)S(1)}, u32[]{:S(2)}, u32[]{:S(2)}) collective-permute-start(f32[1,64,256]{2,1,0:T(8,128)S(1)} %add.190), channel_id=1, source_target_pairs={{0,16},{8,24},{16,0},{24,8},{1,17},{9,25},{17,1},{25,9},{2,18},{10... | collective-permute-start | bytes 196616 | tf_op jit(solution)/shard_map/cond/branch_1_fun/ppermute | solution.py:292
  28.1 1.2 %collective-permute-start.9 = (f32[2,64,256]{2,1,0:T(8,128)S(1)}, f32[2,64,256]{2,1,0:T(8,128)S(1)}, u32[]{:S(2)}, u32[]{:S(2)}) collective-permute-start(f32[2,64,256]{2,1,0:T(8,128)S(1)} %add.181), channel_id=1, source_target_pairs={{0,16},{8,24},{16,0},{24,8},{1,17},{9,25},{17,1},{25,9},{2,18},{10... | collective-permute-start | bytes 393224 | tf_op jit(solution)/shard_map/cond/branch_1_fun/ppermute | solution.py:292
  29.3 1.1 %collective-permute-start.14 = (f32[1,64,256]{2,1,0:T(8,128)S(1)}, f32[1,64,256]{2,1,0:T(8,128)S(1)}, u32[]{:S(2)}, u32[]{:S(2)}) collective-permute-start(f32[1,64,256]{2,1,0:T(8,128)S(1)} %add_divide_fusion.5.refs_0_), channel_id=1, source_target_pairs={{0,16},{8,24},{16,0},{24,8},{1,17},{9,25},{17,1},{25,9},{2,18},{10... | collective-permute-start | bytes 196616 | tf_op jit(solution)/shard_map/cond/branch_1_fun/ppermute | solution.py:292
  30.4 2.1 %collective-permute-done.7 = f32[2,64,256]{2,1,0:T(8,128)S(1)} collective-permute-done((f32[2,64,256]{2,1,0:T(8,128)S(1)}, f32[2,64,256]{2,1,0:T(8,128)S(1)}, u32[]{:S(2)}, u32[]{:S(2)}) %collective-permute-start.7) | collective-permute-done | bytes 131104 | tf_op jit(solution)/shard_map/cond/branch_1_fun/ppermute | solution.py:295
  32.5 1.7 %collective-permute-done.9 = f32[2,64,256]{2,1,0:T(8,128)S(1)} collective-permute-done((f32[2,64,256]{2,1,0:T(8,128)S(1)}, f32[2,64,256]{2,1,0:T(8,128)S(1)}, u32[]{:S(2)}, u32[]{:S(2)}) %collective-permute-start.9) | collective-permute-done | bytes 131104 | tf_op jit(solution)/shard_map/cond/branch_1_fun/ppermute | solution.py:292
  34.3 1.6 %collective-permute-start.10 = (f32[2,64,256]{2,1,0:T(8,128)S(1)}, f32[2,64,256]{2,1,0:T(8,128)S(1)}, u32[]{:S(2)}, u32[]{:S(2)}) collective-permute-start(f32[2,64,256]{2,1,0:T(8,128)S(1)} %get-tuple-element.379.fa), channel_id=1, source_target_pairs={{0,16},{8,24},{16,0},{24,8},{1,17},{9,25},{17,1},{25,9},{2,18},{10... | collective-permute-start | bytes 393224 | tf_op jit(solution)/shard_map/cond/branch_1_fun/ppermute | solution.py:292
  36.5 1.4 %collective-permute-start.17 = (f32[1,64,256]{2,1,0:T(8,128)S(1)}, f32[1,64,256]{2,1,0:T(8,128)S(1)}, u32[]{:S(2)}, u32[]{:S(2)}) collective-permute-start(f32[1,64,256]{2,1,0:T(8,128)S(1)} %add_divide_fusion.4.refs_1_), channel_id=1, source_target_pairs={{0,8},{8,0},{16,24},{24,16},{1,9},{9,1},{17,25},{25,17},{2,10},{10... | collective-permute-start | bytes 196616 | tf_op jit(solution)/shard_map/cond/branch_1_fun/ppermute | solution.py:295
  38.0 2.0 %branch_1_fun.6 = (f32[72,128]{1,0:T(8,128)S(1)}, bf16[3,12,256,256]{3,2,1,0:T(8,128)(2,1)}) custom-call(), custom_call_target="tpu_custom_call" | custom-call | tf_op jit(solution)/shard_map/cond/branch_1_fun/pallas_call | solution.py:323
  40.6 0.9 %collective-permute-done.17.fb = f32[1,64,256]{2,1,0:T(8,128)S(1)} collective-permute-done((f32[1,64,256]{2,1,0:T(8,128)S(1)}, f32[1,64,256]{2,1,0:T(8,128)S(1)}, u32[]{:S(2)}, u32[]{:S(2)}) %collective-permute-start.17) | collective-permute-done | bytes 65568 | tf_op jit(solution)/shard_map/cond/branch_1_fun/ppermute | solution.py:295
  42.2 1.3 %branch_1_fun.9 = (bf16[3,2,256,256]{3,2,1,0:T(8,128)(2,1)S(1)}, f32[72,128]{1,0:T(8,128)S(1)}, bf16[3,12,256,256]{3,2,1,0:T(8,128)(2,1)}) custom-call(s32[2]{0:T(128)S(1)} %get-tuple-element.171.place, bf16[3,12,256,256]{3,2,1,0:T(8,128)(2,1)S(1)} %get-tuple-element.172.trips, ...), custom_call_target="tpu_custom_call", output_to_operand_aliasing={{2}: (10, {})} | custom-call | tf_op jit(solution)/shard_map/cond/branch_1_fun/pallas_call | solution.py:356
  43.7 28.0 %collective-permute-start.76 = (f32[72,128]{1,0:T(8,128)S(1)}, f32[72,128]{1,0:T(8,128)S(1)}, u32[]{:S(2)}, u32[]{:S(2)}) collective-permute-start(f32[72,128]{1,0:T(8,128)S(1)} %get-tuple-element.367), channel_id=1, source_target_pairs={{0,6},{1,7},{2,4},{3,5},{4,2},{5,3},{6,0},{7,1},{8,14},{9,15},{10,... | collective-permute-start | bytes 110600 | tf_op jit(solution)/shard_map/ppermute | solution.py:372
  72.4 0.9 %shard_map.71 = bf16[3,12,256,256]{3,2,1,0:T(8,128)(2,1)} custom-call(bf16[3,2,256,256]{3,2,1,0:T(8,128)(2,1)S(1)} %get-tuple-element.368.local, bf16[3,12,256,256]{3,2,1,0:T(8,128)(2,1)} %get-tuple-element.369.before), custom_call_target="tpu_custom_call", output_to_operand_aliasing={{}: (1, {})} | custom-call | tf_op jit(solution)/shard_map/pallas_call | solution.py:451
  73.7 2.9 %collective-permute-done.77 = f32[72,128]{1,0:T(8,128)S(1)} collective-permute-done((f32[72,128]{1,0:T(8,128)S(1)}, f32[72,128]{1,0:T(8,128)S(1)}, u32[]{:S(2)}, u32[]{:S(2)}) %collective-permute-start.77) | collective-permute-done | bytes 36896 | tf_op jit(solution)/shard_map/ppermute | solution.py:372
  76.7 1.4 %collective-permute-done.79.refs_2_ = f32[4,72,128]{2,1,0:T(8,128)S(1)} collective-permute-done((f32[4,72,128]{2,1,0:T(8,128)S(1)}, f32[4,72,128]{2,1,0:T(8,128)S(1)}, u32[]{:S(2)}, u32[]{:S(2)}) %collective-permute-start.79) | collective-permute-done | bytes 147488 | tf_op jit(solution)/shard_map/ppermute | solution.py:372
  78.1 1.5 %shard_map.72 = f32[3,4096]{1,0:T(4,128)} custom-call(s32[2]{0:T(128)S(1)} %pad_add_fusion.place, f32[3,4096]{1,0:T(4,128)S(1)} %get-tuple-element.371.span, f32[8,12,128]{2,1,0:T(8,128)S(1)} %get-tuple-element.372.refs_0_, f32[4,72,128]{2,1,0:T(8,128)S(1)} %pad_maximum_fusion.1.refs_1_, f32[4,72,128]{2,1,0:T(8,128)S(1)} %collective-permute-done.79.refs_2_), custom_call_target="tpu_custom_call" | custom-call | tf_op jit(solution)/shard_map/pallas_call | solution.py:461
  (47 shorter events, 8.5 us)
Async XLA Ops:
  0.6 10.2 %copy-start.2 = (s32[12]{0:T(128)S(1)}, s32[12]{0:T(128)}, u32[]{:S(2)}) copy-start(s32[12]{0:T(128)} %cols.1) | copy-start | bytes 148
  0.6 10.2 %copy-start.1 = (f32[3,32768]{1,0:T(4,128)S(1)}, f32[3,32768]{1,0:T(4,128)}, u32[]{:S(2)}) copy-start(f32[3,32768]{1,0:T(4,128)} %dest.1) | copy-start | bytes 1179652
  0.7 10.2 %copy-start = (bf16[12,256,256]{2,1,0:T(8,128)(2,1)S(1)}, bf16[12,256,256]{2,1,0:T(8,128)(2,1)}, u32[]{:S(2)}) copy-start(bf16[12,256,256]{2,1,0:T(8,128)(2,1)} %target.1) | copy-start | bytes 4718596
  5.0 7.2 %collective-permute-start.72 = (f32[84,128]{1,0:T(8,128)S(1)}, f32[84,128]{1,0:T(8,128)S(1)}, u32[]{:S(2)}, u32[]{:S(2)}) collective-permute-start(f32[84,128]{1,0:T(8,128)S(1)} %get-tuple-element.348), channel_id=1, source_target_pairs={{0,6},{1,7},{2,4},{3,5},{4,2},{5,3},{6,0},{7,1},{8,14},{9,15},{10,... | collective-permute-start | bytes 129032 | tf_op jit(solution)/shard_map/ppermute | solution.py:372
  10.2 4.9 %collective-permute-start.73 = (f32[84,128]{1,0:T(8,128)S(1)}, f32[84,128]{1,0:T(8,128)S(1)}, u32[]{:S(2)}, u32[]{:S(2)}) collective-permute-start(f32[84,128]{1,0:T(8,128)S(1)} %get-tuple-element.348), channel_id=1, source_target_pairs={{0,4},{1,5},{2,6},{3,7},{4,0},{5,1},{6,2},{7,3},{8,12},{9,13},{10,... | collective-permute-start | bytes 129032 | tf_op jit(solution)/shard_map/ppermute | solution.py:372
  10.2 4.9 %collective-permute-start.74 = (f32[84,128]{1,0:T(8,128)S(1)}, f32[84,128]{1,0:T(8,128)S(1)}, u32[]{:S(2)}, u32[]{:S(2)}) collective-permute-start(f32[84,128]{1,0:T(8,128)S(1)} %get-tuple-element.348), channel_id=1, source_target_pairs={{0,2},{1,3},{2,0},{3,1},{4,6},{5,7},{6,4},{7,5},{8,10},{9,11},{10,... | collective-permute-start | bytes 129032 | tf_op jit(solution)/shard_map/ppermute | solution.py:372
  15.1 1.5 %collective-permute-start.75 = (f32[4,84,128]{2,1,0:T(8,128)S(1)}, f32[4,84,128]{2,1,0:T(8,128)S(1)}, u32[]{:S(2)}, u32[]{:S(2)}) collective-permute-start(f32[4,84,128]{2,1,0:T(8,128)S(1)} %pad_maximum_fusion.refs_0_), channel_id=1, source_target_pairs={{0,1},{1,0},{2,3},{3,2},{4,5},{5,4},{6,7},{7,6},{8,9},{9,8},{10,11... | collective-permute-start | bytes 516104 | tf_op jit(solution)/shard_map/ppermute | solution.py:372
  18.1 4.9 %collective-permute-start.12 = (f32[1,64,256]{2,1,0:T(8,128)S(1)}, f32[1,64,256]{2,1,0:T(8,128)S(1)}, u32[]{:S(2)}, u32[]{:S(2)}) collective-permute-start(f32[1,64,256]{2,1,0:T(8,128)S(1)} %slice.53), channel_id=1, source_target_pairs={{0,16},{8,24},{16,0},{24,8},{1,17},{9,25},{17,1},{25,9},{2,18},{10... | collective-permute-start | bytes 196616 | tf_op jit(solution)/shard_map/cond/branch_1_fun/ppermute | solution.py:292
  19.7 6.1 %collective-permute-start.15 = (f32[1,64,256]{2,1,0:T(8,128)S(1)}, f32[1,64,256]{2,1,0:T(8,128)S(1)}, u32[]{:S(2)}, u32[]{:S(2)}) collective-permute-start(f32[1,64,256]{2,1,0:T(8,128)S(1)} %slice.60), channel_id=1, source_target_pairs={{0,8},{8,0},{16,24},{24,16},{1,9},{9,1},{17,25},{25,17},{2,10},{10... | collective-permute-start | bytes 196616 | tf_op jit(solution)/shard_map/cond/branch_1_fun/ppermute | solution.py:295
  21.2 6.2 %collective-permute-start.6 = (f32[2,64,256]{2,1,0:T(8,128)S(1)}, f32[2,64,256]{2,1,0:T(8,128)S(1)}, u32[]{:S(2)}, u32[]{:S(2)}) collective-permute-start(f32[2,64,256]{2,1,0:T(8,128)S(1)} %get-tuple-element.177), channel_id=1, source_target_pairs={{0,16},{8,24},{16,0},{24,8},{1,17},{9,25},{17,1},{25,9},{2,18},{10... | collective-permute-start | bytes 393224 | tf_op jit(solution)/shard_map/cond/branch_1_fun/ppermute | solution.py:292
  21.7 6.3 %collective-permute-start.8 = (f32[2,64,256]{2,1,0:T(8,128)S(1)}, f32[2,64,256]{2,1,0:T(8,128)S(1)}, u32[]{:S(2)}, u32[]{:S(2)}) collective-permute-start(f32[2,64,256]{2,1,0:T(8,128)S(1)} %get-tuple-element.181), channel_id=1, source_target_pairs={{0,8},{8,0},{16,24},{24,16},{1,9},{9,1},{17,25},{25,17},{2,10},{10... | collective-permute-start | bytes 393224 | tf_op jit(solution)/shard_map/cond/branch_1_fun/ppermute | solution.py:295
  23.0 6.3 %collective-permute-start.13 = (f32[1,64,256]{2,1,0:T(8,128)S(1)}, f32[1,64,256]{2,1,0:T(8,128)S(1)}, u32[]{:S(2)}, u32[]{:S(2)}) collective-permute-start(f32[1,64,256]{2,1,0:T(8,128)S(1)} %add.184), channel_id=1, source_target_pairs={{0,8},{8,0},{16,24},{24,16},{1,9},{9,1},{17,25},{25,17},{2,10},{10... | collective-permute-start | bytes 196616 | tf_op jit(solution)/shard_map/cond/branch_1_fun/ppermute | solution.py:295
  25.8 10.7 %collective-permute-start.16 = (f32[1,64,256]{2,1,0:T(8,128)S(1)}, f32[1,64,256]{2,1,0:T(8,128)S(1)}, u32[]{:S(2)}, u32[]{:S(2)}) collective-permute-start(f32[1,64,256]{2,1,0:T(8,128)S(1)} %add.190), channel_id=1, source_target_pairs={{0,16},{8,24},{16,0},{24,8},{1,17},{9,25},{17,1},{25,9},{2,18},{10... | collective-permute-start | bytes 196616 | tf_op jit(solution)/shard_map/cond/branch_1_fun/ppermute | solution.py:292
  27.4 5.0 %collective-permute-start.7 = (f32[2,64,256]{2,1,0:T(8,128)S(1)}, f32[2,64,256]{2,1,0:T(8,128)S(1)}, u32[]{:S(2)}, u32[]{:S(2)}) collective-permute-start(f32[2,64,256]{2,1,0:T(8,128)S(1)} %add.177), channel_id=1, source_target_pairs={{0,8},{8,0},{16,24},{24,16},{1,9},{9,1},{17,25},{25,17},{2,10},{10... | collective-permute-start | bytes 393224 | tf_op jit(solution)/shard_map/cond/branch_1_fun/ppermute | solution.py:295
  28.1 6.1 %collective-permute-start.9 = (f32[2,64,256]{2,1,0:T(8,128)S(1)}, f32[2,64,256]{2,1,0:T(8,128)S(1)}, u32[]{:S(2)}, u32[]{:S(2)}) collective-permute-start(f32[2,64,256]{2,1,0:T(8,128)S(1)} %add.181), channel_id=1, source_target_pairs={{0,16},{8,24},{16,0},{24,8},{1,17},{9,25},{17,1},{25,9},{2,18},{10... | collective-permute-start | bytes 393224 | tf_op jit(solution)/shard_map/cond/branch_1_fun/ppermute | solution.py:292
  29.3 11.3 %collective-permute-start.14 = (f32[1,64,256]{2,1,0:T(8,128)S(1)}, f32[1,64,256]{2,1,0:T(8,128)S(1)}, u32[]{:S(2)}, u32[]{:S(2)}) collective-permute-start(f32[1,64,256]{2,1,0:T(8,128)S(1)} %add_divide_fusion.5.refs_0_), channel_id=1, source_target_pairs={{0,16},{8,24},{16,0},{24,8},{1,17},{9,25},{17,1},{25,9},{2,18},{10... | collective-permute-start | bytes 196616 | tf_op jit(solution)/shard_map/cond/branch_1_fun/ppermute | solution.py:292
  34.3 7.9 %collective-permute-start.10 = (f32[2,64,256]{2,1,0:T(8,128)S(1)}, f32[2,64,256]{2,1,0:T(8,128)S(1)}, u32[]{:S(2)}, u32[]{:S(2)}) collective-permute-start(f32[2,64,256]{2,1,0:T(8,128)S(1)} %get-tuple-element.379.fa), channel_id=1, source_target_pairs={{0,16},{8,24},{16,0},{24,8},{1,17},{9,25},{17,1},{25,9},{2,18},{10... | collective-permute-start | bytes 393224 | tf_op jit(solution)/shard_map/cond/branch_1_fun/ppermute | solution.py:292
  35.8 6.3 %collective-permute-start.11 = (f32[2,64,256]{2,1,0:T(8,128)S(1)}, f32[2,64,256]{2,1,0:T(8,128)S(1)}, u32[]{:S(2)}, u32[]{:S(2)}) collective-permute-start(f32[2,64,256]{2,1,0:T(8,128)S(1)} %get-tuple-element.378.fb), channel_id=1, source_target_pairs={{0,8},{8,0},{16,24},{24,16},{1,9},{9,1},{17,25},{25,17},{2,10},{10... | collective-permute-start | bytes 393224 | tf_op jit(solution)/shard_map/cond/branch_1_fun/ppermute | solution.py:295
  36.5 5.0 %collective-permute-start.17 = (f32[1,64,256]{2,1,0:T(8,128)S(1)}, f32[1,64,256]{2,1,0:T(8,128)S(1)}, u32[]{:S(2)}, u32[]{:S(2)}) collective-permute-start(f32[1,64,256]{2,1,0:T(8,128)S(1)} %add_divide_fusion.4.refs_1_), channel_id=1, source_target_pairs={{0,8},{8,0},{16,24},{24,16},{1,9},{9,1},{17,25},{25,17},{2,10},{10... | collective-permute-start | bytes 196616 | tf_op jit(solution)/shard_map/cond/branch_1_fun/ppermute | solution.py:295
  43.7 29.9 %collective-permute-start.76 = (f32[72,128]{1,0:T(8,128)S(1)}, f32[72,128]{1,0:T(8,128)S(1)}, u32[]{:S(2)}, u32[]{:S(2)}) collective-permute-start(f32[72,128]{1,0:T(8,128)S(1)} %get-tuple-element.367), channel_id=1, source_target_pairs={{0,6},{1,7},{2,4},{3,5},{4,2},{5,3},{6,0},{7,1},{8,14},{9,15},{10,... | collective-permute-start | bytes 110600 | tf_op jit(solution)/shard_map/ppermute | solution.py:372
  71.7 4.9 %collective-permute-start.77 = (f32[72,128]{1,0:T(8,128)S(1)}, f32[72,128]{1,0:T(8,128)S(1)}, u32[]{:S(2)}, u32[]{:S(2)}) collective-permute-start(f32[72,128]{1,0:T(8,128)S(1)} %get-tuple-element.367), channel_id=1, source_target_pairs={{0,4},{1,5},{2,6},{3,7},{4,0},{5,1},{6,2},{7,3},{8,12},{9,13},{10,... | collective-permute-start | bytes 110600 | tf_op jit(solution)/shard_map/ppermute | solution.py:372
  71.8 4.9 %collective-permute-start.78 = (f32[72,128]{1,0:T(8,128)S(1)}, f32[72,128]{1,0:T(8,128)S(1)}, u32[]{:S(2)}, u32[]{:S(2)}) collective-permute-start(f32[72,128]{1,0:T(8,128)S(1)} %get-tuple-element.367), channel_id=1, source_target_pairs={{0,2},{1,3},{2,0},{3,1},{4,6},{5,7},{6,4},{7,5},{8,10},{9,11},{10,... | collective-permute-start | bytes 110600 | tf_op jit(solution)/shard_map/ppermute | solution.py:372
  76.6 1.4 %collective-permute-start.79 = (f32[4,72,128]{2,1,0:T(8,128)S(1)}, f32[4,72,128]{2,1,0:T(8,128)S(1)}, u32[]{:S(2)}, u32[]{:S(2)}) collective-permute-start(f32[4,72,128]{2,1,0:T(8,128)S(1)} %pad_maximum_fusion.1.refs_1_), channel_id=1, source_target_pairs={{0,1},{1,0},{2,3},{3,2},{4,5},{5,4},{6,7},{7,6},{8,9},{9,8},{10,11... | collective-permute-start | bytes 442376 | tf_op jit(solution)/shard_map/ppermute | solution.py:372

commit v3 on v2

--- a/solution.py
+++ b/solution.py
@@ -45,16 +45,18 @@
     live = [(cols[s] >= 0).astype(F32) for s in range(slots)]
     first.wait()
     for t, r in blocks:
+        at = r // LANES * LANES
         diagonal = (
-            lax.broadcasted_iota(jnp.int32, (rows, side), 0) + r == lax.broadcasted_iota(jnp.int32, (rows, side), 1)
+            lax.broadcasted_iota(jnp.int32, (rows, LANES), 0) + (r - at)
+            == lax.broadcasted_iota(jnp.int32, (rows, LANES), 1)
         )
-        column = jnp.sum(jnp.where(diagonal, margins[t : t + 1, :], 0.0), axis=1, keepdims=True)
+        column = jnp.sum(jnp.where(diagonal, margins[t : t + 1, at : at + LANES], 0.0), axis=1, keepdims=True)
         acol[t, r : r + rows, :] = jnp.broadcast_to(column, (rows, LANES))
 
     def row_totals(t, r):
         total = None
         for s in range(slots):
-            part = local[t, s, r : r + rows, :].astype(F32) * live[s]
+            part = (local[t, s, r : r + rows, :] * live[s].astype(local.dtype)).astype(F32)
             total = part if total is None else total + part
         return jnp.sum(total, axis=1, keepdims=True)
 

time: 79.8 us -> 79.7 us (level)
  no operation moved by 1% of the time
where the time goes in v3:
time: 79.7 us; the launch traced here: 79.5 us
  starting transfers between devices  48.4 us (61%)
  Pallas kernels  14 us (18%)
  waiting for transfers between devices  13.7 us (17%)
  between operations  1.37 us (2%)
  loops' own time  1.01 us (1%)
    ppermute x8, starting transfers between devices, swap(): return lax.ppermute(y, 'orig', [(i, i ^ k) for i in range(n)])  34.6 us
    ppermute x8, waiting for transfers between devices, swap(): return lax.ppermute(y, 'orig', [(i, i ^ k) for i in range(n)])  9.03 us
    ppermute x6, starting transfers between devices, over_first(): return lax.ppermute(x, 'tm', [(i, i ^ 2) for i in range(4)])  7.55 us
    ppermute x6, starting transfers between devices, over_second(): return lax.ppermute(x, 'tm', [(i, i ^ 1) for i in range(4)])  6.27 us
    pallas_call x1, Pallas kernels, on_device(): pl.pallas_call(functools.partial(anchor_kernel, starts=[sum((n for _, n i...  4.13 us
    ppermute x6, waiting for transfers between devices, over_second(): return lax.ppermute(x, 'tm', [(i, i ^ 1) for i in range(4)])  2.97 us
    pallas_call x1, Pallas kernels, cycle(): pl.pallas_call(functools.partial(empty_kernel, empty=empty), compiler_par...  2.01 us
    ppermute x6, waiting for transfers between devices, over_first(): return lax.ppermute(x, 'tm', [(i, i ^ 2) for i in range(4)])  1.73 us
  transfers between devices with their start and end apart: 20, of which 10 were waited for; matrix products, arithmetic and copies ran while one was open for 1% of the time, Pallas kernels for 7%

profile of v3, /device:TPU:0, one launch (start us, length us, event | category | flops | bytes accessed | tf_op | source)
XLA Modules:
  0.0 79.5 jit_solution(5148291929521647137)
XLA Ops:
  0.7 4.1 %shard_map.68 = (bf16[3,12,256,256]{3,2,1,0:T(8,128)(2,1)S(1)}, f32[3,256,128]{2,1,0:T(8,128)S(1)}, f32[84,128]{1,0:T(8,128)S(1)}, s32[1]{0:T(128)}) custom-call(s32[2]{0:T(128)S(1)} %pad_add_fusion.place, s32[12]{0:T(128)} %cols.1, f32[3,256]{1,0:T(4,128)} %anchor.1, bf16[3,12,256,256]{3,2,1,0:T(8,128)(2,1)} %trips.1), custom_call_target="tpu_custom_call" | custom-call | tf_op jit(solution)/shard_map/pallas_call | solution.py:396
  4.9 5.1 %collective-permute-start.72 = (f32[84,128]{1,0:T(8,128)S(1)}, f32[84,128]{1,0:T(8,128)S(1)}, u32[]{:S(2)}, u32[]{:S(2)}) collective-permute-start(f32[84,128]{1,0:T(8,128)S(1)} %get-tuple-element.348), channel_id=1, source_target_pairs={{0,6},{1,7},{2,4},{3,5},{4,2},{5,3},{6,0},{7,1},{8,14},{9,15},{10,... | collective-permute-start | bytes 129032 | tf_op jit(solution)/shard_map/ppermute | solution.py:374
  12.0 2.9 %collective-permute-done.73 = f32[84,128]{1,0:T(8,128)S(1)} collective-permute-done((f32[84,128]{1,0:T(8,128)S(1)}, f32[84,128]{1,0:T(8,128)S(1)}, u32[]{:S(2)}, u32[]{:S(2)}) %collective-permute-start.73) | collective-permute-done | bytes 43040 | tf_op jit(solution)/shard_map/ppermute | solution.py:374
  15.7 0.8 collective-permute-done.75.refs_1_
  16.5 1.5 %shard_map.70 = (f32[6,12,128]{2,1,0:T(8,128)S(1)}, f32[8,12,128]{2,1,0:T(8,128)S(1)}, f32[2,64,256]{2,1,0:T(8,128)S(1)}, f32[2,64,256]{2,1,0:T(8,128)S(1)}, f32...) custom-call(s32[2]{0:T(128)S(1)} %pad_add_fusion.place, ...), custom_call_target="tpu_custom_call" | custom-call | tf_op jit(solution)/shard_map/pallas_call | solution.py:424
  17.9 25.7 %conditional.1 = (bf16[3,12,256,256]{3,2,1,0:T(8,128)(2,1)}, bf16[3,2,256,256]{3,2,1,0:T(8,128)(2,1)S(1)}, f32[72,128]{1,0:T(8,128)S(1)}) conditional(s32[]{:T(128)} %bitcast.3, (s32[2]{0:T(128)S(1)}, bf16[3,12,256,256]{3,2,1,0:T(8,128)(2,1)S(1)}, f32[3,256,128]{2,1,0:T(8,128)S(1)}, f32[6,12,128]{2,1,0:T(8,128)S(1)}, ...), branch_computations={%region_0.0_spmd, %region_1.0_spmd, %region_2.0_spmd, %region_3.0_... | conditional | flops 1572888 | bytes 29922172 | solution.py:442
  18.0 1.6 %collective-permute-start.12 = (f32[1,64,256]{2,1,0:T(8,128)S(1)}, f32[1,64,256]{2,1,0:T(8,128)S(1)}, u32[]{:S(2)}, u32[]{:S(2)}) collective-permute-start(f32[1,64,256]{2,1,0:T(8,128)S(1)} %slice.53), channel_id=1, source_target_pairs={{0,16},{8,24},{16,0},{24,8},{1,17},{9,25},{17,1},{25,9},{2,18},{10... | collective-permute-start | bytes 196616 | tf_op jit(solution)/shard_map/cond/branch_1_fun/ppermute | solution.py:294
  19.6 1.5 %collective-permute-start.15 = (f32[1,64,256]{2,1,0:T(8,128)S(1)}, f32[1,64,256]{2,1,0:T(8,128)S(1)}, u32[]{:S(2)}, u32[]{:S(2)}) collective-permute-start(f32[1,64,256]{2,1,0:T(8,128)S(1)} %slice.60), channel_id=1, source_target_pairs={{0,8},{8,0},{16,24},{24,16},{1,9},{9,1},{17,25},{25,17},{2,10},{10... | collective-permute-start | bytes 196616 | tf_op jit(solution)/shard_map/cond/branch_1_fun/ppermute | solution.py:297
  22.9 1.6 %collective-permute-start.13 = (f32[1,64,256]{2,1,0:T(8,128)S(1)}, f32[1,64,256]{2,1,0:T(8,128)S(1)}, u32[]{:S(2)}, u32[]{:S(2)}) collective-permute-start(f32[1,64,256]{2,1,0:T(8,128)S(1)} %add.184), channel_id=1, source_target_pairs={{0,8},{8,0},{16,24},{24,16},{1,9},{9,1},{17,25},{25,17},{2,10},{10... | collective-permute-start | bytes 196616 | tf_op jit(solution)/shard_map/cond/branch_1_fun/ppermute | solution.py:297
  25.7 1.6 %collective-permute-start.16 = (f32[1,64,256]{2,1,0:T(8,128)S(1)}, f32[1,64,256]{2,1,0:T(8,128)S(1)}, u32[]{:S(2)}, u32[]{:S(2)}) collective-permute-start(f32[1,64,256]{2,1,0:T(8,128)S(1)} %add.190), channel_id=1, source_target_pairs={{0,16},{8,24},{16,0},{24,8},{1,17},{9,25},{17,1},{25,9},{2,18},{10... | collective-permute-start | bytes 196616 | tf_op jit(solution)/shard_map/cond/branch_1_fun/ppermute | solution.py:294
  27.9 1.2 %collective-permute-start.9 = (f32[2,64,256]{2,1,0:T(8,128)S(1)}, f32[2,64,256]{2,1,0:T(8,128)S(1)}, u32[]{:S(2)}, u32[]{:S(2)}) collective-permute-start(f32[2,64,256]{2,1,0:T(8,128)S(1)} %add.181), channel_id=1, source_target_pairs={{0,16},{8,24},{16,0},{24,8},{1,17},{9,25},{17,1},{25,9},{2,18},{10... | collective-permute-start | bytes 393224 | tf_op jit(solution)/shard_map/cond/branch_1_fun/ppermute | solution.py:294
  29.2 1.1 %collective-permute-start.14 = (f32[1,64,256]{2,1,0:T(8,128)S(1)}, f32[1,64,256]{2,1,0:T(8,128)S(1)}, u32[]{:S(2)}, u32[]{:S(2)}) collective-permute-start(f32[1,64,256]{2,1,0:T(8,128)S(1)} %add_divide_fusion.5.refs_0_), channel_id=1, source_target_pairs={{0,16},{8,24},{16,0},{24,8},{1,17},{9,25},{17,1},{25,9},{2,18},{10... | collective-permute-start | bytes 196616 | tf_op jit(solution)/shard_map/cond/branch_1_fun/ppermute | solution.py:294
  30.3 2.1 %collective-permute-done.7 = f32[2,64,256]{2,1,0:T(8,128)S(1)} collective-permute-done((f32[2,64,256]{2,1,0:T(8,128)S(1)}, f32[2,64,256]{2,1,0:T(8,128)S(1)}, u32[]{:S(2)}, u32[]{:S(2)}) %collective-permute-start.7) | collective-permute-done | bytes 131104 | tf_op jit(solution)/shard_map/cond/branch_1_fun/ppermute | solution.py:297
  32.3 1.7 %collective-permute-done.9 = f32[2,64,256]{2,1,0:T(8,128)S(1)} collective-permute-done((f32[2,64,256]{2,1,0:T(8,128)S(1)}, f32[2,64,256]{2,1,0:T(8,128)S(1)}, u32[]{:S(2)}, u32[]{:S(2)}) %collective-permute-start.9) | collective-permute-done | bytes 131104 | tf_op jit(solution)/shard_map/cond/branch_1_fun/ppermute | solution.py:294
  34.1 1.6 %collective-permute-start.10 = (f32[2,64,256]{2,1,0:T(8,128)S(1)}, f32[2,64,256]{2,1,0:T(8,128)S(1)}, u32[]{:S(2)}, u32[]{:S(2)}) collective-permute-start(f32[2,64,256]{2,1,0:T(8,128)S(1)} %get-tuple-element.379.fa), channel_id=1, source_target_pairs={{0,16},{8,24},{16,0},{24,8},{1,17},{9,25},{17,1},{25,9},{2,18},{10... | collective-permute-start | bytes 393224 | tf_op jit(solution)/shard_map/cond/branch_1_fun/ppermute | solution.py:294
  36.4 1.4 %collective-permute-start.17 = (f32[1,64,256]{2,1,0:T(8,128)S(1)}, f32[1,64,256]{2,1,0:T(8,128)S(1)}, u32[]{:S(2)}, u32[]{:S(2)}) collective-permute-start(f32[1,64,256]{2,1,0:T(8,128)S(1)} %add_divide_fusion.4.refs_1_), channel_id=1, source_target_pairs={{0,8},{8,0},{16,24},{24,16},{1,9},{9,1},{17,25},{25,17},{2,10},{10... | collective-permute-start | bytes 196616 | tf_op jit(solution)/shard_map/cond/branch_1_fun/ppermute | solution.py:297
  37.8 2.0 %branch_1_fun.6 = (f32[72,128]{1,0:T(8,128)S(1)}, bf16[3,12,256,256]{3,2,1,0:T(8,128)(2,1)}) custom-call(), custom_call_target="tpu_custom_call" | custom-call | tf_op jit(solution)/shard_map/cond/branch_1_fun/pallas_call | solution.py:325
  40.5 0.9 %collective-permute-done.17.fb = f32[1,64,256]{2,1,0:T(8,128)S(1)} collective-permute-done((f32[1,64,256]{2,1,0:T(8,128)S(1)}, f32[1,64,256]{2,1,0:T(8,128)S(1)}, u32[]{:S(2)}, u32[]{:S(2)}) %collective-permute-start.17) | collective-permute-done | bytes 65568 | tf_op jit(solution)/shard_map/cond/branch_1_fun/ppermute | solution.py:297
  42.0 1.3 %branch_1_fun.9 = (bf16[3,2,256,256]{3,2,1,0:T(8,128)(2,1)S(1)}, f32[72,128]{1,0:T(8,128)S(1)}, bf16[3,12,256,256]{3,2,1,0:T(8,128)(2,1)}) custom-call(s32[2]{0:T(128)S(1)} %get-tuple-element.171.place, bf16[3,12,256,256]{3,2,1,0:T(8,128)(2,1)S(1)} %get-tuple-element.172.trips, ...), custom_call_target="tpu_custom_call", output_to_operand_aliasing={{2}: (10, {})} | custom-call | tf_op jit(solution)/shard_map/cond/branch_1_fun/pallas_call | solution.py:358
  43.6 28.0 %collective-permute-start.76 = (f32[72,128]{1,0:T(8,128)S(1)}, f32[72,128]{1,0:T(8,128)S(1)}, u32[]{:S(2)}, u32[]{:S(2)}) collective-permute-start(f32[72,128]{1,0:T(8,128)S(1)} %get-tuple-element.367), channel_id=1, source_target_pairs={{0,6},{1,7},{2,4},{3,5},{4,2},{5,3},{6,0},{7,1},{8,14},{9,15},{10,... | collective-permute-start | bytes 110600 | tf_op jit(solution)/shard_map/ppermute | solution.py:374
  72.3 0.9 %shard_map.71 = bf16[3,12,256,256]{3,2,1,0:T(8,128)(2,1)} custom-call(bf16[3,2,256,256]{3,2,1,0:T(8,128)(2,1)S(1)} %get-tuple-element.368.local, bf16[3,12,256,256]{3,2,1,0:T(8,128)(2,1)} %get-tuple-element.369.before), custom_call_target="tpu_custom_call", output_to_operand_aliasing={{}: (1, {})} | custom-call | tf_op jit(solution)/shard_map/pallas_call | solution.py:453
  73.6 2.9 %collective-permute-done.77 = f32[72,128]{1,0:T(8,128)S(1)} collective-permute-done((f32[72,128]{1,0:T(8,128)S(1)}, f32[72,128]{1,0:T(8,128)S(1)}, u32[]{:S(2)}, u32[]{:S(2)}) %collective-permute-start.77) | collective-permute-done | bytes 36896 | tf_op jit(solution)/shard_map/ppermute | solution.py:374
  76.6 1.4 %collective-permute-done.79.refs_2_ = f32[4,72,128]{2,1,0:T(8,128)S(1)} collective-permute-done((f32[4,72,128]{2,1,0:T(8,128)S(1)}, f32[4,72,128]{2,1,0:T(8,128)S(1)}, u32[]{:S(2)}, u32[]{:S(2)}) %collective-permute-start.79) | collective-permute-done | bytes 147488 | tf_op jit(solution)/shard_map/ppermute | solution.py:374
  77.9 1.5 %shard_map.72 = f32[3,4096]{1,0:T(4,128)} custom-call(s32[2]{0:T(128)S(1)} %pad_add_fusion.place, f32[3,4096]{1,0:T(4,128)S(1)} %get-tuple-element.371.span, f32[8,12,128]{2,1,0:T(8,128)S(1)} %get-tuple-element.372.refs_0_, f32[4,72,128]{2,1,0:T(8,128)S(1)} %pad_maximum_fusion.1.refs_1_, f32[4,72,128]{2,1,0:T(8,128)S(1)} %collective-permute-done.79.refs_2_), custom_call_target="tpu_custom_call" | custom-call | tf_op jit(solution)/shard_map/pallas_call | solution.py:463
  (47 shorter events, 8.5 us)
Async XLA Ops:
  0.6 10.0 %copy-start.2 = (s32[12]{0:T(128)S(1)}, s32[12]{0:T(128)}, u32[]{:S(2)}) copy-start(s32[12]{0:T(128)} %cols.1) | copy-start | bytes 148
  0.6 10.0 %copy-start.1 = (f32[3,32768]{1,0:T(4,128)S(1)}, f32[3,32768]{1,0:T(4,128)}, u32[]{:S(2)}) copy-start(f32[3,32768]{1,0:T(4,128)} %dest.1) | copy-start | bytes 1179652
  0.7 10.0 %copy-start = (bf16[12,256,256]{2,1,0:T(8,128)(2,1)S(1)}, bf16[12,256,256]{2,1,0:T(8,128)(2,1)}, u32[]{:S(2)}) copy-start(bf16[12,256,256]{2,1,0:T(8,128)(2,1)} %target.1) | copy-start | bytes 4718596
  4.9 7.2 %collective-permute-start.72 = (f32[84,128]{1,0:T(8,128)S(1)}, f32[84,128]{1,0:T(8,128)S(1)}, u32[]{:S(2)}, u32[]{:S(2)}) collective-permute-start(f32[84,128]{1,0:T(8,128)S(1)} %get-tuple-element.348), channel_id=1, source_target_pairs={{0,6},{1,7},{2,4},{3,5},{4,2},{5,3},{6,0},{7,1},{8,14},{9,15},{10,... | collective-permute-start | bytes 129032 | tf_op jit(solution)/shard_map/ppermute | solution.py:374
  10.0 4.9 %collective-permute-start.73 = (f32[84,128]{1,0:T(8,128)S(1)}, f32[84,128]{1,0:T(8,128)S(1)}, u32[]{:S(2)}, u32[]{:S(2)}) collective-permute-start(f32[84,128]{1,0:T(8,128)S(1)} %get-tuple-element.348), channel_id=1, source_target_pairs={{0,4},{1,5},{2,6},{3,7},{4,0},{5,1},{6,2},{7,3},{8,12},{9,13},{10,... | collective-permute-start | bytes 129032 | tf_op jit(solution)/shard_map/ppermute | solution.py:374
  10.0 4.9 %collective-permute-start.74 = (f32[84,128]{1,0:T(8,128)S(1)}, f32[84,128]{1,0:T(8,128)S(1)}, u32[]{:S(2)}, u32[]{:S(2)}) collective-permute-start(f32[84,128]{1,0:T(8,128)S(1)} %get-tuple-element.348), channel_id=1, source_target_pairs={{0,2},{1,3},{2,0},{3,1},{4,6},{5,7},{6,4},{7,5},{8,10},{9,11},{10,... | collective-permute-start | bytes 129032 | tf_op jit(solution)/shard_map/ppermute | solution.py:374
  15.0 1.5 %collective-permute-start.75 = (f32[4,84,128]{2,1,0:T(8,128)S(1)}, f32[4,84,128]{2,1,0:T(8,128)S(1)}, u32[]{:S(2)}, u32[]{:S(2)}) collective-permute-start(f32[4,84,128]{2,1,0:T(8,128)S(1)} %pad_maximum_fusion.refs_0_), channel_id=1, source_target_pairs={{0,1},{1,0},{2,3},{3,2},{4,5},{5,4},{6,7},{7,6},{8,9},{9,8},{10,11... | collective-permute-start | bytes 516104 | tf_op jit(solution)/shard_map/ppermute | solution.py:374
  18.0 4.9 %collective-permute-start.12 = (f32[1,64,256]{2,1,0:T(8,128)S(1)}, f32[1,64,256]{2,1,0:T(8,128)S(1)}, u32[]{:S(2)}, u32[]{:S(2)}) collective-permute-start(f32[1,64,256]{2,1,0:T(8,128)S(1)} %slice.53), channel_id=1, source_target_pairs={{0,16},{8,24},{16,0},{24,8},{1,17},{9,25},{17,1},{25,9},{2,18},{10... | collective-permute-start | bytes 196616 | tf_op jit(solution)/shard_map/cond/branch_1_fun/ppermute | solution.py:294
  19.6 6.1 %collective-permute-start.15 = (f32[1,64,256]{2,1,0:T(8,128)S(1)}, f32[1,64,256]{2,1,0:T(8,128)S(1)}, u32[]{:S(2)}, u32[]{:S(2)}) collective-permute-start(f32[1,64,256]{2,1,0:T(8,128)S(1)} %slice.60), channel_id=1, source_target_pairs={{0,8},{8,0},{16,24},{24,16},{1,9},{9,1},{17,25},{25,17},{2,10},{10... | collective-permute-start | bytes 196616 | tf_op jit(solution)/shard_map/cond/branch_1_fun/ppermute | solution.py:297
  21.1 6.2 %collective-permute-start.6 = (f32[2,64,256]{2,1,0:T(8,128)S(1)}, f32[2,64,256]{2,1,0:T(8,128)S(1)}, u32[]{:S(2)}, u32[]{:S(2)}) collective-permute-start(f32[2,64,256]{2,1,0:T(8,128)S(1)} %get-tuple-element.177), channel_id=1, source_target_pairs={{0,16},{8,24},{16,0},{24,8},{1,17},{9,25},{17,1},{25,9},{2,18},{10... | collective-permute-start | bytes 393224 | tf_op jit(solution)/shard_map/cond/branch_1_fun/ppermute | solution.py:294
  21.6 6.3 %collective-permute-start.8 = (f32[2,64,256]{2,1,0:T(8,128)S(1)}, f32[2,64,256]{2,1,0:T(8,128)S(1)}, u32[]{:S(2)}, u32[]{:S(2)}) collective-permute-start(f32[2,64,256]{2,1,0:T(8,128)S(1)} %get-tuple-element.181), channel_id=1, source_target_pairs={{0,8},{8,0},{16,24},{24,16},{1,9},{9,1},{17,25},{25,17},{2,10},{10... | collective-permute-start | bytes 393224 | tf_op jit(solution)/shard_map/cond/branch_1_fun/ppermute | solution.py:297
  22.9 6.3 %collective-permute-start.13 = (f32[1,64,256]{2,1,0:T(8,128)S(1)}, f32[1,64,256]{2,1,0:T(8,128)S(1)}, u32[]{:S(2)}, u32[]{:S(2)}) collective-permute-start(f32[1,64,256]{2,1,0:T(8,128)S(1)} %add.184), channel_id=1, source_target_pairs={{0,8},{8,0},{16,24},{24,16},{1,9},{9,1},{17,25},{25,17},{2,10},{10... | collective-permute-start | bytes 196616 | tf_op jit(solution)/shard_map/cond/branch_1_fun/ppermute | solution.py:297
  25.7 10.7 %collective-permute-start.16 = (f32[1,64,256]{2,1,0:T(8,128)S(1)}, f32[1,64,256]{2,1,0:T(8,128)S(1)}, u32[]{:S(2)}, u32[]{:S(2)}) collective-permute-start(f32[1,64,256]{2,1,0:T(8,128)S(1)} %add.190), channel_id=1, source_target_pairs={{0,16},{8,24},{16,0},{24,8},{1,17},{9,25},{17,1},{25,9},{2,18},{10... | collective-permute-start | bytes 196616 | tf_op jit(solution)/shard_map/cond/branch_1_fun/ppermute | solution.py:294
  27.3 5.0 %collective-permute-start.7 = (f32[2,64,256]{2,1,0:T(8,128)S(1)}, f32[2,64,256]{2,1,0:T(8,128)S(1)}, u32[]{:S(2)}, u32[]{:S(2)}) collective-permute-start(f32[2,64,256]{2,1,0:T(8,128)S(1)} %add.177), channel_id=1, source_target_pairs={{0,8},{8,0},{16,24},{24,16},{1,9},{9,1},{17,25},{25,17},{2,10},{10... | collective-permute-start | bytes 393224 | tf_op jit(solution)/shard_map/cond/branch_1_fun/ppermute | solution.py:297
  27.9 6.1 %collective-permute-start.9 = (f32[2,64,256]{2,1,0:T(8,128)S(1)}, f32[2,64,256]{2,1,0:T(8,128)S(1)}, u32[]{:S(2)}, u32[]{:S(2)}) collective-permute-start(f32[2,64,256]{2,1,0:T(8,128)S(1)} %add.181), channel_id=1, source_target_pairs={{0,16},{8,24},{16,0},{24,8},{1,17},{9,25},{17,1},{25,9},{2,18},{10... | collective-permute-start | bytes 393224 | tf_op jit(solution)/shard_map/cond/branch_1_fun/ppermute | solution.py:294
  29.2 11.3 %collective-permute-start.14 = (f32[1,64,256]{2,1,0:T(8,128)S(1)}, f32[1,64,256]{2,1,0:T(8,128)S(1)}, u32[]{:S(2)}, u32[]{:S(2)}) collective-permute-start(f32[1,64,256]{2,1,0:T(8,128)S(1)} %add_divide_fusion.5.refs_0_), channel_id=1, source_target_pairs={{0,16},{8,24},{16,0},{24,8},{1,17},{9,25},{17,1},{25,9},{2,18},{10... | collective-permute-start | bytes 196616 | tf_op jit(solution)/shard_map/cond/branch_1_fun/ppermute | solution.py:294
  34.1 7.9 %collective-permute-start.10 = (f32[2,64,256]{2,1,0:T(8,128)S(1)}, f32[2,64,256]{2,1,0:T(8,128)S(1)}, u32[]{:S(2)}, u32[]{:S(2)}) collective-permute-start(f32[2,64,256]{2,1,0:T(8,128)S(1)} %get-tuple-element.379.fa), channel_id=1, source_target_pairs={{0,16},{8,24},{16,0},{24,8},{1,17},{9,25},{17,1},{25,9},{2,18},{10... | collective-permute-start | bytes 393224 | tf_op jit(solution)/shard_map/cond/branch_1_fun/ppermute | solution.py:294
  35.7 6.3 %collective-permute-start.11 = (f32[2,64,256]{2,1,0:T(8,128)S(1)}, f32[2,64,256]{2,1,0:T(8,128)S(1)}, u32[]{:S(2)}, u32[]{:S(2)}) collective-permute-start(f32[2,64,256]{2,1,0:T(8,128)S(1)} %get-tuple-element.378.fb), channel_id=1, source_target_pairs={{0,8},{8,0},{16,24},{24,16},{1,9},{9,1},{17,25},{25,17},{2,10},{10... | collective-permute-start | bytes 393224 | tf_op jit(solution)/shard_map/cond/branch_1_fun/ppermute | solution.py:297
  36.4 5.0 %collective-permute-start.17 = (f32[1,64,256]{2,1,0:T(8,128)S(1)}, f32[1,64,256]{2,1,0:T(8,128)S(1)}, u32[]{:S(2)}, u32[]{:S(2)}) collective-permute-start(f32[1,64,256]{2,1,0:T(8,128)S(1)} %add_divide_fusion.4.refs_1_), channel_id=1, source_target_pairs={{0,8},{8,0},{16,24},{24,16},{1,9},{9,1},{17,25},{25,17},{2,10},{10... | collective-permute-start | bytes 196616 | tf_op jit(solution)/shard_map/cond/branch_1_fun/ppermute | solution.py:297
  43.6 29.9 %collective-permute-start.76 = (f32[72,128]{1,0:T(8,128)S(1)}, f32[72,128]{1,0:T(8,128)S(1)}, u32[]{:S(2)}, u32[]{:S(2)}) collective-permute-start(f32[72,128]{1,0:T(8,128)S(1)} %get-tuple-element.367), channel_id=1, source_target_pairs={{0,6},{1,7},{2,4},{3,5},{4,2},{5,3},{6,0},{7,1},{8,14},{9,15},{10,... | collective-permute-start | bytes 110600 | tf_op jit(solution)/shard_map/ppermute | solution.py:374
  71.6 4.9 %collective-permute-start.77 = (f32[72,128]{1,0:T(8,128)S(1)}, f32[72,128]{1,0:T(8,128)S(1)}, u32[]{:S(2)}, u32[]{:S(2)}) collective-permute-start(f32[72,128]{1,0:T(8,128)S(1)} %get-tuple-element.367), channel_id=1, source_target_pairs={{0,4},{1,5},{2,6},{3,7},{4,0},{5,1},{6,2},{7,3},{8,12},{9,13},{10,... | collective-permute-start | bytes 110600 | tf_op jit(solution)/shard_map/ppermute | solution.py:374
  71.6 4.9 %collective-permute-start.78 = (f32[72,128]{1,0:T(8,128)S(1)}, f32[72,128]{1,0:T(8,128)S(1)}, u32[]{:S(2)}, u32[]{:S(2)}) collective-permute-start(f32[72,128]{1,0:T(8,128)S(1)} %get-tuple-element.367), channel_id=1, source_target_pairs={{0,2},{1,3},{2,0},{3,1},{4,6},{5,7},{6,4},{7,5},{8,10},{9,11},{10,... | collective-permute-start | bytes 110600 | tf_op jit(solution)/shard_map/ppermute | solution.py:374
  76.5 1.4 %collective-permute-start.79 = (f32[4,72,128]{2,1,0:T(8,128)S(1)}, f32[4,72,128]{2,1,0:T(8,128)S(1)}, u32[]{:S(2)}, u32[]{:S(2)}) collective-permute-start(f32[4,72,128]{2,1,0:T(8,128)S(1)} %pad_maximum_fusion.1.refs_1_), channel_id=1, source_target_pairs={{0,1},{1,0},{2,3},{3,2},{4,5},{5,4},{6,7},{7,6},{8,9},{9,8},{10,11... | collective-permute-start | bytes 442376 | tf_op jit(solution)/shard_map/ppermute | solution.py:374
